TPU v7x, 128 devices: a whole 4x4x4 slice. The times are simulated.
128 devices in a mesh: lat: 4 (over z), lon: 32 (over x, y, core).
Axes of the slice: x: 4, y: 4, z: 4, core: 2. Of those that a mesh axis runs over, the one named last changes fastest.
Arguments:
- spectrum: float32 [1296, 32, 8192], P(None, 'lat', 'lon'), may hold values from 0.01 to 1
- sea_mask: int32 [32, 8192], P('lat', 'lon'), may hold values 0 or 1
- courant: float32 [2, 1296], replicated, may hold values from -0.45 to 0.45
- obs_tile: int32 [32768, 1], P(('lat', 'lon')), may hold values from 0 to 127; in each aligned block of 256 rows (0 to 255, 256 to 511, ...) at most 8 rows name the same one
- obs_cell: int32 [32768], P(('lat', 'lon')), may hold values from 0 to 2047
- obs_value: float32 [32768], P(('lat', 'lon')), may hold values from 1 to 3
- obs_error: float32 [32768], P(('lat', 'lon')), may hold values from 0.05 to 0.5
Outputs:
- updated: float32 [1296, 32, 8192], P(None, 'lat', 'lon')
- increment: float32 [32, 8192], P('lat', 'lon')
Inputs may be any that keep to these rules, and one draw needn't show every extreme that they name: `obs_tile`: within the 256 reports of one device no tile occurs more than 8 times.
All inputs are finite; a program needn't handle non-finite values. No bound on the sum of `sea_mask` on one device may be relied on, other than what follows from the above.
Results may differ from a plain program's by a relative error of at most 0.00002.
Values sent between devices are 32-bit elements; how exact they have to be, the bound alone decides.
A program may use at most 128 MiB of HBM per device.

v0:
```python
import jax
import jax.numpy as jnp
from jax import lax
from jax.sharding import PartitionSpec as P

PASSES = 8


spread_rate = 0.2
prior_weight = 4.0


def with_halo(array, sides, width):
    edges = {}
    for axis, dim in sides:
        size, length = (lax.axis_size(axis), array.shape[dim])
        up = [(i, (i + 1) % size) for i in range(size)]
        last = lax.slice_in_dim(array, length - width, length, axis=dim)
        leading = lax.slice_in_dim(array, 0, width, axis=dim)
        edges[dim] = (
            lax.ppermute(last, axis, up),
            lax.ppermute(leading, axis, [(b, a) for a, b in up]),
        )
    done = []
    for _, dim in sides:
        low, high = edges[dim]
        around = [(width, width) if d in done else (0, 0) for d in range(array.ndim)]
        array = jnp.concatenate([jnp.pad(low, around), array, jnp.pad(high, around)], axis=dim)
        done.append(dim)
    return array


def with_halo_2(cells, sides, width):
    for axis, dim in sides:
        count = lax.axis_size(axis)
        head = lax.slice_in_dim(cells, 0, width, axis=dim)
        tail = lax.slice_in_dim(cells, cells.shape[dim] - width, cells.shape[dim], axis=dim)
        cells = jnp.concatenate(
            [
                lax.ppermute(tail, axis, [(i, (i + 1) % count) for i in range(count)]),
                cells,
                lax.ppermute(head, axis, [((i + 1) % count, i) for i in range(count)]),
            ],
            axis=dim,
        )
    return cells


def relax_pass(fields, sea_ext):
    centre = fields[:, 1:-1, 1:-1]
    summed = sea_ext[2:, 1:-1] * (fields[:, 2:, 1:-1] - centre)
    summed = summed + sea_ext[:-2, 1:-1] * (fields[:, :-2, 1:-1] - centre)
    summed = summed + sea_ext[1:-1, 2:] * (fields[:, 1:-1, 2:] - centre)
    summed = summed + sea_ext[1:-1, :-2] * (fields[:, 1:-1, :-2] - centre)
    return centre + spread_rate * sea_ext[1:-1, 1:-1] * summed


def body(spectrum, sea_mask, courant, obs_tile, obs_cell, obs_value, obs_error):
    tile_rows, tile_cols = sea_mask.shape
    lat_count = lax.axis_size("lat")
    lon_count = lax.axis_size("lon")
    devices = lat_count * lon_count
    report_count = obs_value.shape[0]
    slot_cap = max(8, 4 * report_count // devices)
    outer_rim = with_halo(spectrum, (("lat", 1), ("lon", 2)), 1)
    height = 4.0 * jnp.sqrt(jnp.mean(spectrum, axis=0))
    height_flat = height.reshape(-1)
    weights = 1.0 / obs_error
    owners = obs_tile[:, 0]
    blank_grid = jnp.zeros((2, tile_rows * tile_cols), jnp.float32)
    position = jnp.arange(report_count, dtype=jnp.int32)
    earlier = (owners[:, None] == owners[None, :]) & (position[None, :] < position[:, None])
    slot_index = jnp.sum(earlier.astype(jnp.int32), axis=1)
    reports = jnp.stack([obs_value, weights, obs_cell.astype(jnp.float32)])
    outbox = (
        jnp.zeros((3, devices, slot_cap), jnp.float32)
        .at[:, owners, slot_index]
        .set(reports)
        .reshape(3, lat_count, lon_count, slot_cap)
    )
    arrived = lax.all_to_all(
        lax.all_to_all(outbox, "lat", split_axis=1, concat_axis=1, tiled=True),
        "lon",
        split_axis=2,
        concat_axis=2,
        tiled=True,
    ).reshape(3, -1)
    totals = blank_grid
    cell_ids = arrived[2].astype(jnp.int32)
    report_weights = arrived[1]
    misfit = report_weights * (arrived[0] - height_flat[cell_ids])
    totals = totals.at[0, cell_ids].add(misfit)
    totals = totals.at[1, cell_ids].add(report_weights)
    ocean = sea_mask.astype(jnp.float32)
    fields = totals.reshape(2, tile_rows, tile_cols) * ocean
    halo_depth = 2
    coast_ext = with_halo_2(sea_mask, (("lat", 0), ("lon", 1)), halo_depth)
    lat_line = (
        lax.axis_index("lat") * tile_rows
        + jnp.arange(tile_rows + 2 * halo_depth, dtype=jnp.int32)
        - halo_depth
    )
    inside = (lat_line >= 0) & (lat_line < lat_count * tile_rows)
    coast_ext = jnp.where(inside[:, None], coast_ext, 0).astype(jnp.float32)
    edge_sea = coast_ext[
        halo_depth - 1 : coast_ext.shape[0] - halo_depth + 1,
        halo_depth - 1 : coast_ext.shape[1] - halo_depth + 1,
    ]
    for repeat in range(PASSES // 2):
        padded = with_halo_2(fields, (("lat", 1), ("lon", 2)), 2)
        fields = relax_pass(relax_pass(padded, coast_ext), edge_sea)
    increment = ocean * fields[0] / (prior_weight + fields[1])
    factor = jnp.exp(2.0 * increment / height)
    rim_scale = with_halo_2(factor, (("lat", 0), ("lon", 1)), 1)
    analyzed = outer_rim * rim_scale
    east_speed = courant[0][:, None, None]
    north_speed = courant[1][:, None, None]
    row_band = analyzed[:, 1:-1, :]
    ocean_band = edge_sea[1:-1, :]
    flux_east = (
        (
            jnp.maximum(east_speed, 0.0) * row_band[:, :, :-1]
            + jnp.minimum(east_speed, 0.0) * row_band[:, :, 1:]
        )
        * ocean_band[:, :-1]
        * ocean_band[:, 1:]
    )
    col_strip = analyzed[:, :, 1:-1]
    ocean_strip = edge_sea[:, 1:-1]
    flux_north = (
        (
            jnp.maximum(north_speed, 0.0) * col_strip[:, :-1]
            + jnp.minimum(north_speed, 0.0) * col_strip[:, 1:]
        )
        * ocean_strip[:-1]
        * ocean_strip[1:]
    )
    centre = analyzed[:, 1:-1, 1:-1]
    updated = ocean * (
        centre
        - (flux_east[:, :, 1:] - flux_east[:, :, :-1])
        - (flux_north[:, 1:] - flux_north[:, :-1])
    )
    return (updated, increment)


def solution(mesh):
    return jax.shard_map(
        body,
        mesh=mesh,
        in_specs=(
            P(None, "lat", "lon"),
            P("lat", "lon"),
            P(),
            P(("lat", "lon"), None),
            P(("lat", "lon")),
            P(("lat", "lon")),
            P(("lat", "lon")),
        ),
        out_specs=(P(None, "lat", "lon"), P("lat", "lon")),
        check_vma=False,
    )
```

profile of v0, /device:TPU:0, one launch (start us, length us, event | category | flops | bytes accessed | tf_op | source)
XLA Modules:
  0.0 245.4 jit_solution(15258800450788764085)
XLA Ops:
  0.7 0.8 fusion.118
  1.5 2.0 collective-permute-start.8
  3.5 2.1 collective-permute-start.9
  5.6 0.7 convert_element_type.30
  6.3 0.7 broadcast_divide_fusion
  7.0 0.9 convert_reduce_fusion
  7.9 0.7 or_select_fusion
  8.6 0.7 maximum_bitcast_fusion
  9.5 11.5 %scatter_fusion = f32[3,128,8]{0,2,1:T(8,128)S(1)} fusion(f32[3,128,8]{0,2,1:T(8,128)S(1)} %broadcast_in_dim.13, s32[256]{0:T(256)S(1)} %bitcast.35, f32[256,3]{1,0:T(8,128)S(1)} %copy.52), kind=kCustom, calls=%fused_computation.1 | custom fusion | bytes 11264 | tf_op jit(solution)/shard_map/scatter | solution.py:78
  21.0 0.3 copy.53
  21.2 0.7 reshape.164
  21.9 3.3 %all-to-all-start = ((f32[4,1,768]{2,1,0:T(1,128)}), f32[4,1,768]{2,1,0:T(1,128)S(1)}, u32[]{:S(2)}, u32[]{:S(2)}) async-start(f32[4,1,768]{2,1,0:T(1,128)} %reshape.164), calls=%async_computation | async-start | bytes 24576 | tf_op jit(solution)/shard_map/all_to_all | solution.py:82
  25.2 4.8 %reduce_sum.22 = f32[8,256]{1,0:T(8,128)S(1)} reduce(f32[1296,8,256]{2,1,0:T(8,128)} %param.7, f32[]{:T(128)} %constant.15.clone.1), dimensions={0}, to_apply=%region_2.3 | reduce | flops 2652160 | bytes 10625028 | tf_op jit(solution)/shard_map/reduce_sum | solution.py:66
  30.2 5.1 %collective-permute-start.11 = (s32[12,2]{1,0:T(8,128)S(1)}, s32[12,2]{1,0:T(8,128)S(1)}, u32[]{:S(2)}, u32[]{:S(2)}) collective-permute-start(s32[12,2]{1,0:T(8,128)S(1)} %get-tuple-element.56), channel_id=1, source_target_pairs={{1,0},{2,1},{3,2},{4,3},{5,4},{6,5},{7,6},{8,7},{9,8},{10,9},{11,1... | collective-permute-start | bytes 296 | tf_op jit(solution)/shard_map/ppermute | solution.py:42
  35.3 0.5 broadcast.222
  35.8 0.7 reduce.16
  36.6 0.8 copy.54
  37.4 4.0 %all-to-all-start.1 = ((f32[3,4,32,8]{3,1,0,2:T(4,128)}), f32[3,4,32,8]{3,1,0,2:T(4,128)S(1)}, u32[]{:S(2)}, u32[]{:S(2)}) async-start(f32[3,4,32,8]{3,1,0,2:T(4,128)} %copy.54), calls=%async_computation.1 | async-start | bytes 393216 | tf_op jit(solution)/shard_map/all_to_all | solution.py:81
  41.5 8.3 %all-to-all-done.1 = f32[3,4,32,8]{3,1,0,2:T(4,128)S(1)} async-done(((f32[3,4,32,8]{3,1,0,2:T(4,128)}), f32[3,4,32,8]{3,1,0,2:T(4,128)S(1)}, u32[]{:S(2)}, u32[]{:S(2)}) %all-to-all-start.1) | async-done | bytes 12320 | tf_op jit(solution)/shard_map/all_to_all | solution.py:81
  50.5 6.2 %gather_fusion = f32[1024]{0:T(1024)S(1)} fusion(f32[2048]{0:T(1024)S(1)} %bitcast.34, s32[1024]{0:T(1024)S(1)} %broadcast_clamp_fusion), kind=kCustom, calls=%fused_computation | custom fusion | bytes 12288 | tf_op jit(solution)/shard_map/gather | solution.py:91
  56.7 6.0 %scatter_custom_fusion.1 = f32[4096]{0:T(1024)S(1)} fusion(s32[1024]{0:T(1024)S(1)} %get-tuple-element.64, f32[1024]{0:T(1024)S(1)} %subtract_multiply_fusion, f32[]{:T(128)} %constant.15.clone.1), kind=kCustom, calls=%fused_computation.182 | custom fusion | flops 1024 | bytes 16388
  62.7 6.1 %scatter_fusion.1 = f32[4096]{0:T(1024)S(1)} fusion(f32[4096]{0:T(1024)S(1)} %scatter_custom_fusion.1, s32[1024]{0:T(1024)S(1)} %get-tuple-element.63, f32[1024]{0:T(1024)S(1)} %reshape.154), kind=kCustom, calls=%fused_computation.3 | custom fusion | flops 1024 | bytes 16384
  68.9 3.8 %collective-permute-start.4 = (f32[2,2,256]{2,1,0:T(2,128)S(1)}, f32[2,2,256]{2,1,0:T(2,128)S(1)}, u32[]{:S(2)}, u32[]{:S(2)}) collective-permute-start(f32[2,2,256]{2,1,0:T(2,128)S(1)} %get-tuple-element.57), channel_id=1, source_target_pairs={{0,32},{32,64},{64,96},{96,0},{1,33},{33,65},{65,97},{97,1},{2,34}... | collective-permute-start | bytes 12296 | tf_op jit(solution)/shard_map/ppermute | solution.py:40
  72.7 1.3 collective-permute-start.5
  74.1 1.4 collective-permute-done.4
  75.5 0.8 collective-permute-done.5
  76.4 0.9 collective-permute-start.7
  77.3 1.4 collective-permute-done.7
  78.7 5.0 %collective-permute-done.6 = f32[2,12,2]{2,1,0:T(8,128)S(1)} collective-permute-done((f32[2,12,2]{2,1,0:T(8,128)S(1)}, f32[2,12,2]{2,1,0:T(8,128)S(1)}, u32[]{:S(2)}, u32[]{:S(2)}) %collective-permute-start.6) | collective-permute-done | bytes 224 | tf_op jit(solution)/shard_map/ppermute | solution.py:40
  83.9 0.1 fusion.48
  84.1 0.8 collective-permute-start.12
  85.0 2.5 %collective-permute-start.13 = (f32[2,2,256]{2,1,0:T(2,128)S(1)}, f32[2,2,256]{2,1,0:T(2,128)S(1)}, u32[]{:S(2)}, u32[]{:S(2)}) collective-permute-start(f32[2,2,256]{2,1,0:T(2,128)S(1)} %get-tuple-element.54), channel_id=1, source_target_pairs={{32,0},{64,32},{96,64},{0,96},{33,1},{65,33},{97,65},{1,97},{34,2}... | collective-permute-start | bytes 12296 | tf_op jit(solution)/shard_map/ppermute | solution.py:42
  87.4 9.2 %fusion.102 = (f32[1296,1,256]{2,1,0:T(1,128)S(1)}, f32[1296,1,256]{2,1,0:T(1,128)S(1)}) fusion(f32[1296,8,256]{2,1,0:T(8,128)} %param.7), kind=kLoop, calls=%fused_computation.205 | loop fusion | bytes 5308416 | tf_op jit(solution)/shard_map/slice | solution.py:18
  96.7 1.1 collective-permute-start.2
  98.0 0.5 collective-permute-start.14
  98.6 1.2 collective-permute-start.1
  99.8 4.8 %collective-permute-done.14 = f32[2,12,2]{2,1,0:T(8,128)S(1)} collective-permute-done((f32[2,12,2]{2,1,0:T(8,128)S(1)}, f32[2,12,2]{2,1,0:T(8,128)S(1)}, u32[]{:S(2)}, u32[]{:S(2)}) %collective-permute-start.14) | collective-permute-done | bytes 224 | tf_op jit(solution)/shard_map/ppermute | solution.py:40
  104.6 0.1 fusion.37
  104.9 1.0 collective-permute-start.16
  105.9 2.3 collective-permute-start.17
  108.2 7.5 %fusion.103 = (f32[1296,8,1]{2,1,0:T(8,128)}, f32[1296,8,1]{2,1,0:T(8,128)}) fusion(f32[1296,8,256]{2,1,0:T(8,128)} %param.7), kind=kLoop, calls=%fused_computation.206 | loop fusion | bytes 165888 | tf_op jit(solution)/shard_map/slice | solution.py:18
  115.7 15.5 %collective-permute-done.16 = f32[2,2,256]{2,1,0:T(2,128)S(1)} collective-permute-done((f32[2,2,256]{2,1,0:T(2,128)S(1)}, f32[2,2,256]{2,1,0:T(2,128)S(1)}, u32[]{:S(2)}, u32[]{:S(2)}) %collective-permute-start.16) | collective-permute-done | bytes 4128 | tf_op jit(solution)/shard_map/ppermute | solution.py:40
  131.3 0.5 collective-permute-start.18
  131.8 4.1 %copy.63 = f32[1296,8,1]{0,1,2:T(8,128)S(1)} copy(f32[1296,8,1]{2,1,0:T(8,128)} %get-tuple-element.21) | data formatting | bytes 82944
  135.9 4.7 %collective-permute-start.3 = (f32[1296,8,1]{0,1,2:T(8,128)S(1)}, f32[1296,8,1]{0,1,2:T(8,128)S(1)}, u32[]{:S(2)}, u32[]{:S(2)}) collective-permute-start(f32[1296,8,1]{0,1,2:T(8,128)S(1)} %copy.63), channel_id=1, source_target_pairs={{1,0},{2,1},{3,2},{4,3},{5,4},{6,5},{7,6},{8,7},{9,8},{10,9},{11,1... | collective-permute-start | bytes 124424 | tf_op jit(solution)/shard_map/ppermute | solution.py:22
  140.8 0.1 fusion.26
  141.1 3.2 %collective-permute-start.21 = (f32[2,2,256]{2,1,0:T(2,128)S(1)}, f32[2,2,256]{2,1,0:T(2,128)S(1)}, u32[]{:S(2)}, u32[]{:S(2)}) collective-permute-start(f32[2,2,256]{2,1,0:T(2,128)S(1)} %get-tuple-element.50), channel_id=1, source_target_pairs={{32,0},{64,32},{96,64},{0,96},{33,1},{65,33},{97,65},{1,97},{34,2}... | collective-permute-start | bytes 12296 | tf_op jit(solution)/shard_map/ppermute | solution.py:42
  144.4 12.4 %copy.47 = f32[1296,8,256]{0,2,1:T(8,128)} copy(f32[1296,8,256]{2,1,0:T(8,128)} %param.7) | data formatting | bytes 21233664 | tf_op args[0]
  156.8 4.1 %copy.60 = f32[1296,8,1]{0,1,2:T(8,128)S(1)} copy(f32[1296,8,1]{2,1,0:T(8,128)} %get-tuple-element.20) | data formatting | bytes 82944
  161.0 0.5 collective-permute-start.22
  161.6 0.9 collective-permute-done.23
  162.5 5.1 %collective-permute-done.22 = f32[2,12,2]{2,1,0:T(8,128)S(1)} collective-permute-done((f32[2,12,2]{2,1,0:T(8,128)S(1)}, f32[2,12,2]{2,1,0:T(8,128)S(1)}, u32[]{:S(2)}, u32[]{:S(2)}) %collective-permute-start.22) | collective-permute-done | bytes 224 | tf_op jit(solution)/shard_map/ppermute | solution.py:40
  167.9 0.6 divide_exponential_fusion
  168.6 3.2 %collective-permute-start.25 = (f32[1,256]{1,0:T(1,128)S(1)}, f32[1,256]{1,0:T(1,128)S(1)}, u32[]{:S(2)}, u32[]{:S(2)}) collective-permute-start(f32[1,256]{1,0:T(1,128)S(1)} %get-tuple-element.60), channel_id=1, source_target_pairs={{32,0},{64,32},{96,64},{0,96},{33,1},{65,33},{97,65},{1,97},{34,2}... | collective-permute-start | bytes 3080 | tf_op jit(solution)/shard_map/ppermute | solution.py:42
  171.9 1.5 collective-permute-done.24
  173.5 6.8 %collective-permute-done.26 = f32[10,1]{1,0:T(8,128)S(1)} collective-permute-done((f32[10,1]{1,0:T(8,128)S(1)}, f32[10,1]{1,0:T(8,128)S(1)}, u32[]{:S(2)}, u32[]{:S(2)}) %collective-permute-start.26) | collective-permute-done | bytes 72 | tf_op jit(solution)/shard_map/ppermute | solution.py:40
  180.2 1.4 collective-permute-done.27
  181.8 1.8 copy.48
  183.6 1.8 copy.46
  185.3 14.5 %fusion = f32[1296,10,258]{0,2,1:T(8,128)S(1)} fusion(f32[1296,8,1]{0,2,1:T(1,128)S(1)} %copy.66, f32[1296,8,1]{0,2,1:T(1,128)S(1)} %copy.65, f32[1296,1,256]{0,2,1:T(8,128)S(1)} %copy.48, f32[1296,8,256]{0,2,1:T(8,128)} %copy.47, f32[1296,1,256]{0,2,1:T(8,128)S(1)} %copy.46, f32[10,258]{1,0:T(8,128)S(1)} %pad_maximum_fusion.32), kind=kLoop, calls=%fused_computation.5 | loop fusion | flops 30093120 | bytes 26739024 | tf_op jit(solution)/shard_map/mul | solution.py:115
  199.8 5.9 %fusion.6 = f32[1296,8,257]{0,2,1:T(8,128)} fusion(f32[1296,10,258]{0,2,1:T(8,128)S(1)} %fusion, f32[8,257]{1,0:T(8,128)S(1)} %get-tuple-element.34, f32[8,257]{1,0:T(8,128)S(1)} %get-tuple-element.33, f32[1296]{0:T(1024)S(1)} %get-tuple-element.9, f32[1296]{0:T(1024)S(1)} %get-tuple-element.8), kind=kLoop, calls=%fused_computation.17 | loop fusion | flops 13322880 | bytes 32001728 | tf_op jit(solution)/shard_map/mul | solution.py:121
  205.7 7.3 %fusion.3 = f32[1296,9,256]{0,2,1:T(8,128)} fusion(f32[1296,10,258]{0,2,1:T(8,128)S(1)} %fusion, f32[9,256]{1,0:T(8,128)S(1)} %get-tuple-element.36, f32[9,256]{1,0:T(8,128)S(1)} %get-tuple-element.35, f32[1296]{0:T(1024)S(1)} %get-tuple-element.10, f32[1296]{0:T(1024)S(1)} %get-tuple-element.11), kind=kLoop, calls=%fused_computation.12 | loop fusion | flops 14929920 | bytes 35860608 | tf_op jit(solution)/shard_map/mul | solution.py:131
  213.0 20.2 %fusion.8 = f32[1296,8,256]{0,2,1:T(8,128)} fusion(f32[1296,9,256]{0,2,1:T(8,128)} %fusion.3, f32[1296,8,257]{0,2,1:T(8,128)} %fusion.6, f32[1296,10,258]{0,2,1:T(8,128)S(1)} %fusion, f32[8,256]{1,0:T(8,128)S(1)} %convert_element_type.28), kind=kLoop, calls=%fused_computation.21 | loop fusion | flops 13271040 | bytes 63709184 | tf_op jit(solution)/shard_map/mul | solution.py:139
  233.3 12.1 %copy.59 = f32[1296,8,256]{2,1,0:T(8,128)} copy(f32[1296,8,256]{0,2,1:T(8,128)} %fusion.8) | data formatting | bytes 21233664
  (97 shorter events, 3.5 us)
Async XLA Ops:
  0.6 49.6 %copy-start.3 = (s32[2]{0:T(128)S(1)}, s32[2]{0:T(128)}, u32[]{:S(2)}) copy-start(s32[2]{0:T(128)} %constant.55) | copy-start | bytes 28
  0.6 49.7 %copy-start.2 = (s32[2]{0:T(128)S(1)}, s32[2]{0:T(128)}, u32[]{:S(2)}) copy-start(s32[2]{0:T(128)} %constant.52) | copy-start | bytes 28
  0.7 29.4 %copy-start = (s32[8,256]{1,0:T(8,128)S(1)}, s32[8,256]{1,0:T(8,128)}, u32[]{:S(2)}) copy-start(s32[8,256]{1,0:T(8,128)} %param.8) | copy-start | bytes 24580
  1.5 28.6 %collective-permute-start.8 = (s32[2,256]{1,0:T(2,128)S(1)}, s32[2,256]{1,0:T(2,128)S(1)}, u32[]{:S(2)}, u32[]{:S(2)}) collective-permute-start(s32[2,256]{1,0:T(2,128)S(1)} %get-tuple-element.61), channel_id=1, source_target_pairs={{0,32},{32,64},{64,96},{96,0},{1,33},{33,65},{65,97},{97,1},{2,34}... | collective-permute-start | bytes 6152 | tf_op jit(solution)/shard_map/ppermute | solution.py:40
  3.5 26.6 %collective-permute-start.9 = (s32[2,256]{1,0:T(2,128)S(1)}, s32[2,256]{1,0:T(2,128)S(1)}, u32[]{:S(2)}, u32[]{:S(2)}) collective-permute-start(s32[2,256]{1,0:T(2,128)S(1)} %get-tuple-element.62), channel_id=1, source_target_pairs={{32,0},{64,32},{96,64},{0,96},{33,1},{65,33},{97,65},{1,97},{34,2}... | collective-permute-start | bytes 6152 | tf_op jit(solution)/shard_map/ppermute | solution.py:42
  21.9 13.3 %all-to-all-start = ((f32[4,1,768]{2,1,0:T(1,128)}), f32[4,1,768]{2,1,0:T(1,128)S(1)}, u32[]{:S(2)}, u32[]{:S(2)}) async-start(f32[4,1,768]{2,1,0:T(1,128)} %reshape.164), calls=%async_computation | async-start | bytes 24576 | tf_op jit(solution)/shard_map/all_to_all | solution.py:82
  30.2 11.2 %collective-permute-start.10 = (s32[12,2]{1,0:T(8,128)S(1)}, s32[12,2]{1,0:T(8,128)S(1)}, u32[]{:S(2)}, u32[]{:S(2)}) collective-permute-start(s32[12,2]{1,0:T(8,128)S(1)} %get-tuple-element.55), channel_id=1, source_target_pairs={{0,1},{1,2},{2,3},{3,4},{4,5},{5,6},{6,7},{7,8},{8,9},{9,10},{10,1... | collective-permute-start | bytes 296 | tf_op jit(solution)/shard_map/ppermute | solution.py:40
  30.2 11.2 %collective-permute-start.11 = (s32[12,2]{1,0:T(8,128)S(1)}, s32[12,2]{1,0:T(8,128)S(1)}, u32[]{:S(2)}, u32[]{:S(2)}) collective-permute-start(s32[12,2]{1,0:T(8,128)S(1)} %get-tuple-element.56), channel_id=1, source_target_pairs={{1,0},{2,1},{3,2},{4,3},{5,4},{6,5},{7,6},{8,7},{9,8},{10,9},{11,1... | collective-permute-start | bytes 296 | tf_op jit(solution)/shard_map/ppermute | solution.py:42
  37.4 12.4 %all-to-all-start.1 = ((f32[3,4,32,8]{3,1,0,2:T(4,128)}), f32[3,4,32,8]{3,1,0,2:T(4,128)S(1)}, u32[]{:S(2)}, u32[]{:S(2)}) async-start(f32[3,4,32,8]{3,1,0,2:T(4,128)} %copy.54), calls=%async_computation.1 | async-start | bytes 393216 | tf_op jit(solution)/shard_map/all_to_all | solution.py:81
  68.9 6.6 %collective-permute-start.4 = (f32[2,2,256]{2,1,0:T(2,128)S(1)}, f32[2,2,256]{2,1,0:T(2,128)S(1)}, u32[]{:S(2)}, u32[]{:S(2)}) collective-permute-start(f32[2,2,256]{2,1,0:T(2,128)S(1)} %get-tuple-element.57), channel_id=1, source_target_pairs={{0,32},{32,64},{64,96},{96,0},{1,33},{33,65},{65,97},{97,1},{2,34}... | collective-permute-start | bytes 12296 | tf_op jit(solution)/shard_map/ppermute | solution.py:40
  72.7 3.6 %collective-permute-start.5 = (f32[2,2,256]{2,1,0:T(2,128)S(1)}, f32[2,2,256]{2,1,0:T(2,128)S(1)}, u32[]{:S(2)}, u32[]{:S(2)}) collective-permute-start(f32[2,2,256]{2,1,0:T(2,128)S(1)} %get-tuple-element.58), channel_id=1, source_target_pairs={{32,0},{64,32},{96,64},{0,96},{33,1},{65,33},{97,65},{1,97},{34,2}... | collective-permute-start | bytes 12296 | tf_op jit(solution)/shard_map/ppermute | solution.py:42
  76.4 2.3 collective-permute-start.7
  77.3 6.5 %collective-permute-start.6 = (f32[2,12,2]{2,1,0:T(8,128)S(1)}, f32[2,12,2]{2,1,0:T(8,128)S(1)}, u32[]{:S(2)}, u32[]{:S(2)}) collective-permute-start(f32[2,12,2]{2,1,0:T(8,128)S(1)} %get-tuple-element.32), channel_id=1, source_target_pairs={{0,1},{1,2},{2,3},{3,4},{4,5},{5,6},{6,7},{7,8},{8,9},{9,10},{10,1... | collective-permute-start | bytes 584 | tf_op jit(solution)/shard_map/ppermute | solution.py:40
  84.1 13.8 %collective-permute-start.12 = (f32[2,2,256]{2,1,0:T(2,128)S(1)}, f32[2,2,256]{2,1,0:T(2,128)S(1)}, u32[]{:S(2)}, u32[]{:S(2)}) collective-permute-start(f32[2,2,256]{2,1,0:T(2,128)S(1)} %get-tuple-element.53), channel_id=1, source_target_pairs={{0,32},{32,64},{64,96},{96,0},{1,33},{33,65},{65,97},{97,1},{2,34}... | collective-permute-start | bytes 12296 | tf_op jit(solution)/shard_map/ppermute | solution.py:40
  85.0 12.9 %collective-permute-start.13 = (f32[2,2,256]{2,1,0:T(2,128)S(1)}, f32[2,2,256]{2,1,0:T(2,128)S(1)}, u32[]{:S(2)}, u32[]{:S(2)}) collective-permute-start(f32[2,2,256]{2,1,0:T(2,128)S(1)} %get-tuple-element.54), channel_id=1, source_target_pairs={{32,0},{64,32},{96,64},{0,96},{33,1},{65,33},{97,65},{1,97},{34,2}... | collective-permute-start | bytes 12296 | tf_op jit(solution)/shard_map/ppermute | solution.py:42
  96.7 85.1 %collective-permute-start.2 = (f32[1296,1,256]{2,0,1:T(8,128)S(1)}, f32[1296,1,256]{2,0,1:T(8,128)}, u32[]{:S(2)}, u32[]{:S(2)}) collective-permute-start(f32[1296,1,256]{2,0,1:T(8,128)S(1)} %copy.62), channel_id=1, source_target_pairs={{32,0},{64,32},{96,64},{0,96},{33,1},{65,33},{97,65},{1,97},{34,2}... | collective-permute-start | bytes 3981320 | tf_op jit(solution)/shard_map/ppermute | solution.py:22
  98.0 1.8 collective-permute-start.15
  98.0 6.6 %collective-permute-start.14 = (f32[2,12,2]{2,1,0:T(8,128)S(1)}, f32[2,12,2]{2,1,0:T(8,128)S(1)}, u32[]{:S(2)}, u32[]{:S(2)}) collective-permute-start(f32[2,12,2]{2,1,0:T(8,128)S(1)} %get-tuple-element.30), channel_id=1, source_target_pairs={{0,1},{1,2},{2,3},{3,4},{4,5},{5,6},{6,7},{7,8},{8,9},{9,10},{10,1... | collective-permute-start | bytes 584 | tf_op jit(solution)/shard_map/ppermute | solution.py:40
  98.6 85.0 %collective-permute-start.1 = (f32[1296,1,256]{2,0,1:T(8,128)S(1)}, f32[1296,1,256]{2,0,1:T(8,128)}, u32[]{:S(2)}, u32[]{:S(2)}) collective-permute-start(f32[1296,1,256]{2,0,1:T(8,128)S(1)} %copy.61), channel_id=1, source_target_pairs={{0,32},{32,64},{64,96},{96,0},{1,33},{33,65},{65,97},{97,1},{2,34}... | collective-permute-start | bytes 3981320 | tf_op jit(solution)/shard_map/ppermute | solution.py:21
  104.9 26.3 %collective-permute-start.16 = (f32[2,2,256]{2,1,0:T(2,128)S(1)}, f32[2,2,256]{2,1,0:T(2,128)S(1)}, u32[]{:S(2)}, u32[]{:S(2)}) collective-permute-start(f32[2,2,256]{2,1,0:T(2,128)S(1)} %get-tuple-element.51), channel_id=1, source_target_pairs={{0,32},{32,64},{64,96},{96,0},{1,33},{33,65},{65,97},{97,1},{2,34}... | collective-permute-start | bytes 12296 | tf_op jit(solution)/shard_map/ppermute | solution.py:40
  105.9 38.4 %copy-start.1 = (f32[2,1296]{1,0:T(2,128)S(1)}, f32[2,1296]{1,0:T(2,128)}, u32[]{:S(2)}) copy-start(f32[2,1296]{1,0:T(2,128)} %param.9) | copy-start | bytes 31108
  105.9 25.3 %collective-permute-start.17 = (f32[2,2,256]{2,1,0:T(2,128)S(1)}, f32[2,2,256]{2,1,0:T(2,128)S(1)}, u32[]{:S(2)}, u32[]{:S(2)}) collective-permute-start(f32[2,2,256]{2,1,0:T(2,128)S(1)} %get-tuple-element.52), channel_id=1, source_target_pairs={{32,0},{64,32},{96,64},{0,96},{33,1},{65,33},{97,65},{1,97},{34,2}... | collective-permute-start | bytes 12296 | tf_op jit(solution)/shard_map/ppermute | solution.py:42
  131.3 9.3 %collective-permute-start.19 = (f32[2,12,2]{2,1,0:T(8,128)S(1)}, f32[2,12,2]{2,1,0:T(8,128)S(1)}, u32[]{:S(2)}, u32[]{:S(2)}) collective-permute-start(f32[2,12,2]{2,1,0:T(8,128)S(1)} %get-tuple-element.27), channel_id=1, source_target_pairs={{1,0},{2,1},{3,2},{4,3},{5,4},{6,5},{7,6},{8,7},{9,8},{10,9},{11,1... | collective-permute-start | bytes 584 | tf_op jit(solution)/shard_map/ppermute | solution.py:42
  131.3 9.3 %collective-permute-start.18 = (f32[2,12,2]{2,1,0:T(8,128)S(1)}, f32[2,12,2]{2,1,0:T(8,128)S(1)}, u32[]{:S(2)}, u32[]{:S(2)}) collective-permute-start(f32[2,12,2]{2,1,0:T(8,128)S(1)} %get-tuple-element.28), channel_id=1, source_target_pairs={{0,1},{1,2},{2,3},{3,4},{4,5},{5,6},{6,7},{7,8},{8,9},{9,10},{10,1... | collective-permute-start | bytes 584 | tf_op jit(solution)/shard_map/ppermute | solution.py:40
  135.9 45.7 %collective-permute-start.3 = (f32[1296,8,1]{0,1,2:T(8,128)S(1)}, f32[1296,8,1]{0,1,2:T(8,128)S(1)}, u32[]{:S(2)}, u32[]{:S(2)}) collective-permute-start(f32[1296,8,1]{0,1,2:T(8,128)S(1)} %copy.63), channel_id=1, source_target_pairs={{1,0},{2,1},{3,2},{4,3},{5,4},{6,5},{7,6},{8,7},{9,8},{10,9},{11,1... | collective-permute-start | bytes 124424 | tf_op jit(solution)/shard_map/ppermute | solution.py:22
  141.0 19.9 %collective-permute-start.20 = (f32[2,2,256]{2,1,0:T(2,128)S(1)}, f32[2,2,256]{2,1,0:T(2,128)S(1)}, u32[]{:S(2)}, u32[]{:S(2)}) collective-permute-start(f32[2,2,256]{2,1,0:T(2,128)S(1)} %get-tuple-element.49), channel_id=1, source_target_pairs={{0,32},{32,64},{64,96},{96,0},{1,33},{33,65},{65,97},{97,1},{2,34}... | collective-permute-start | bytes 12296 | tf_op jit(solution)/shard_map/ppermute | solution.py:40
  141.1 19.8 %collective-permute-start.21 = (f32[2,2,256]{2,1,0:T(2,128)S(1)}, f32[2,2,256]{2,1,0:T(2,128)S(1)}, u32[]{:S(2)}, u32[]{:S(2)}) collective-permute-start(f32[2,2,256]{2,1,0:T(2,128)S(1)} %get-tuple-element.50), channel_id=1, source_target_pairs={{32,0},{64,32},{96,64},{0,96},{33,1},{65,33},{97,65},{1,97},{34,2}... | collective-permute-start | bytes 12296 | tf_op jit(solution)/shard_map/ppermute | solution.py:42
  161.0 1.5 collective-permute-start.23
  161.0 6.6 %collective-permute-start.22 = (f32[2,12,2]{2,1,0:T(8,128)S(1)}, f32[2,12,2]{2,1,0:T(8,128)S(1)}, u32[]{:S(2)}, u32[]{:S(2)}) collective-permute-start(f32[2,12,2]{2,1,0:T(8,128)S(1)} %get-tuple-element.26), channel_id=1, source_target_pairs={{0,1},{1,2},{2,3},{3,4},{4,5},{5,6},{6,7},{7,8},{8,9},{9,10},{10,1... | collective-permute-start | bytes 584 | tf_op jit(solution)/shard_map/ppermute | solution.py:40
  168.6 4.8 %collective-permute-start.24 = (f32[1,256]{1,0:T(1,128)S(1)}, f32[1,256]{1,0:T(1,128)S(1)}, u32[]{:S(2)}, u32[]{:S(2)}) collective-permute-start(f32[1,256]{1,0:T(1,128)S(1)} %get-tuple-element.59), channel_id=1, source_target_pairs={{0,32},{32,64},{64,96},{96,0},{1,33},{33,65},{65,97},{97,1},{2,34}... | collective-permute-start | bytes 3080 | tf_op jit(solution)/shard_map/ppermute | solution.py:40
  168.6 4.8 %collective-permute-start.25 = (f32[1,256]{1,0:T(1,128)S(1)}, f32[1,256]{1,0:T(1,128)S(1)}, u32[]{:S(2)}, u32[]{:S(2)}) collective-permute-start(f32[1,256]{1,0:T(1,128)S(1)} %get-tuple-element.60), channel_id=1, source_target_pairs={{32,0},{64,32},{96,64},{0,96},{33,1},{65,33},{97,65},{1,97},{34,2}... | collective-permute-start | bytes 3080 | tf_op jit(solution)/shard_map/ppermute | solution.py:42
  173.3 8.4 %collective-permute-start = (f32[1296,8,1]{0,1,2:T(8,128)S(1)}, f32[1296,8,1]{0,1,2:T(8,128)S(1)}, u32[]{:S(2)}, u32[]{:S(2)}) collective-permute-start(f32[1296,8,1]{0,1,2:T(8,128)S(1)} %copy.60), channel_id=1, source_target_pairs={{0,1},{1,2},{2,3},{3,4},{4,5},{5,6},{6,7},{7,8},{8,9},{9,10},{10,1... | collective-permute-start | bytes 124424 | tf_op jit(solution)/shard_map/ppermute | solution.py:21
  173.4 6.8 %collective-permute-start.26 = (f32[10,1]{1,0:T(8,128)S(1)}, f32[10,1]{1,0:T(8,128)S(1)}, u32[]{:S(2)}, u32[]{:S(2)}) collective-permute-start(f32[10,1]{1,0:T(8,128)S(1)} %get-tuple-element.47), channel_id=1, source_target_pairs={{0,1},{1,2},{2,3},{3,4},{4,5},{5,6},{6,7},{7,8},{8,9},{9,10},{10,1... | collective-permute-start | bytes 128 | tf_op jit(solution)/shard_map/ppermute | solution.py:40
  180.2 1.4 collective-permute-start.27
where the time goes:
time: 247 us; the launch traced here: 245 us
  local copies, waits for them, and re-layouts  75.3 us (30%)
  other arithmetic  71.8 us (29%)
  waiting for transfers between devices  52.8 us (21%)
  starting transfers between devices  44.3 us (18%)
    ppermute x12, waiting for transfers between devices, with_halo_2(): lax.ppermute(tail, axis, [(i, (i + 1) % count) for i in range(count)])  40.1 us
    unnamed x20, local copies, waits for them, and re-layouts  33.9 us
    ppermute x12, starting transfers between devices, with_halo_2(): lax.ppermute(head, axis, [((i + 1) % count, i) for i in range(count)])  20.7 us
    mul x1, other arithmetic, body(): ocean * (centre - (flux_east[:, :, 1:] - flux_east[:, :, :-1]) - (flux_no...  20.2 us
    slice x2, local copies, waits for them, and re-layouts, with_halo(): last = lax.slice_in_dim(array, length - width, length, axis=dim)  16.7 us
    mul x1, other arithmetic, body(): analyzed = outer_rim * rim_scale  14.5 us
    unnamed x6, other arithmetic  12.3 us
    scatter x1, local copies, waits for them, and re-layouts, body(): outbox = jnp.zeros((3, devices, slot_cap), jnp.float32).at[:, owners, slo...  11.5 us
  transfers between devices with their start and end apart: 30, of which 12 were waited for; matrix products, arithmetic and copies ran while one was open for 27% of the time, Pallas kernels for 0%

commit v1 on v0

v1 whole, which is shorter than its diff:
```python
import functools

import jax
import jax.numpy as jnp
from jax import lax
from jax.experimental import pallas as pl
from jax.experimental.pallas import tpu as pltpu
from jax.sharding import PartitionSpec as P

SPEC = 1296
ROWS = 8
COLS = 256
LAT = 4
LON = 32
DEV = LAT * LON
NROW = LAT * ROWS
PASSES = 8
LANES = 128
GROUPS = 11
EXT = 384
RIM = 9
CHUNK = 64
CAP_HALF = 704
CAP_ALL = 1344
BLOCK = 72

spread_rate = 0.2
prior_weight = 4.0

f32 = jnp.float32
i32 = jnp.int32
bf16 = jnp.bfloat16
MESH = pl.DeviceIdType.MESH
NT = (((1,), (1,)), ((), ()))
NN = (((1,), (0,)), ((), ()))


def thirds(x):
    high = x.astype(bf16)
    rest = x - high.astype(f32)
    mid = rest.astype(bf16)
    low = (rest - mid.astype(f32)).astype(bf16)
    return high, mid, low


def exchange_kernel(
    cap,
    picks,
    spectrum,
    reports,
    sea,
    tables,
    from_south,
    from_north,
    cols_west,
    cols_east,
    cells,
    outbox,
    inbox,
    turned,
    fields,
    near_west,
    near_east,
    own_west,
    own_east,
    padded,
    going_north,
    going_south,
    load_sems,
    box_sems,
    lat_sems,
    col_sems,
    rim_sems,
    row_sems,
):
    lat = lax.axis_index("lat")
    lon = lax.axis_index("lon")
    me = lat * LON + lon
    west = lax.rem(lon + LON - 1, LON)
    east = lax.rem(lon + 1, LON)

    def load(group):
        size = min(LANES, SPEC - group * LANES)
        part = pl.ds(group * LANES, size)
        return pltpu.make_async_copy(
            spectrum.at[part], cells.at[part], load_sems.at[group]
        )

    for group in range(GROUPS):
        load(group).start()

    barrier = pltpu.get_barrier_semaphore()

    def greet(step, carry):
        peer = lax.rem(me + step, DEV)
        pl.semaphore_signal(
            barrier,
            inc=1,
            device_id=(peer // LON, lax.rem(peer, LON)),
            device_id_type=MESH,
        )
        return carry

    lax.fori_loop(1, DEV, greet, 0)

    owner = reports[0:1, :].astype(i32)
    owner_lat = lax.shift_right_logical(owner, 5)
    owner_lon = lax.bitwise_and(owner, 31)
    tiles = lax.broadcasted_iota(i32, (DEV, 256), 0)
    hit = jnp.where(tiles == owner, 1.0, 0.0)
    before = jnp.where(
        lax.broadcasted_iota(i32, (256, 256), 0)
        < lax.broadcasted_iota(i32, (256, 256), 1),
        1.0,
        0.0,
    )
    earlier = lax.dot_general(
        hit.astype(bf16), before.astype(bf16), NN, preferred_element_type=f32
    )
    rank = jnp.sum(hit * earlier, axis=0, keepdims=True).astype(i32)
    slot = owner_lat * 8 + rank
    slots = lax.broadcasted_iota(i32, (32, 256), 0)
    in_slot = slots == slot
    to_lon = jnp.where(slots == owner_lon, 1.0, 0.0).astype(bf16)
    zero = jnp.zeros((32, 256), f32)
    spread = jnp.concatenate(
        [jnp.where(in_slot, reports[v : v + 1, :], zero) for v in (1, 2, 3)] + [zero],
        axis=0,
    )
    packed = jnp.zeros((LON, LANES), f32)
    for piece in thirds(spread):
        packed = packed + lax.dot_general(
            to_lon, piece, NT, preferred_element_type=f32
        )
    outbox[...] = packed

    lane = lax.broadcasted_iota(i32, (ROWS, LANES), 1)
    blank = jnp.zeros((ROWS, LANES), f32)
    sums = tuple(blank for _ in range(8))
    for group in range(GROUPS):
        load(group).wait()
        size = min(LANES, SPEC - group * LANES)

        def gather(turn, carry, group=group):
            sums, first, final = list(carry[0]), carry[1], carry[2]
            for u in range(4):
                at = turn * 4 + u
                left = cells[group * LANES + at, :, 0:LANES]
                right = cells[group * LANES + at, :, LANES:COLS]
                sums[2 * u] = sums[2 * u] + left
                sums[2 * u + 1] = sums[2 * u + 1] + right
                here = lane == at
                first = jnp.where(here, pltpu.roll(left, at, 1), first)
                final = jnp.where(
                    here, pltpu.roll(right, lax.rem(at + 1, LANES), 1), final
                )
            return tuple(sums), first, final

        sums, first, final = lax.fori_loop(
            0, size // 4, gather, (sums, blank, blank)
        )
        own_west[group] = first
        own_east[group] = final
    left = (sums[0] + sums[2]) + (sums[4] + sums[6])
    right = (sums[1] + sums[3]) + (sums[5] + sums[7])
    here_rows = pl.ds(pl.multiple_of(lat * ROWS, ROWS), ROWS)
    fields[2, here_rows, 0:LANES] = 4.0 * jnp.sqrt(left / SPEC)
    fields[2, here_rows, LANES:COLS] = 4.0 * jnp.sqrt(right / SPEC)
    fields[3, here_rows, 0:COLS] = sea[...].astype(f32)

    pl.semaphore_wait(barrier, DEV - 1)

    def post(step, carry):
        peer = lax.rem(me + step, DEV)
        pltpu.make_async_remote_copy(
            src_ref=outbox.at[pl.ds(lax.rem(peer, LON), 1)],
            dst_ref=inbox.at[pl.ds(me, 1)],
            send_sem=box_sems.at[0],
            recv_sem=box_sems.at[1],
            device_id=(peer // LON, lax.rem(peer, LON)),
            device_id_type=MESH,
        ).start()
        return carry

    lax.fori_loop(1, DEV, post, 0)
    inbox[pl.ds(me, 1), :] = outbox[pl.ds(lon, 1), :]

    def pick(base, turn):
        for u in range(8):
            at = base + turn * 8 + u
            going_north[pl.ds(at, 1), :] = cells[picks[0, at], ROWS - 1 : ROWS, :]
            going_south[pl.ds(at, 1), :] = cells[picks[1, at], 0:1, :]

    def pick_chunk(number):
        base = pl.multiple_of(number * CHUNK, CHUNK)
        lax.fori_loop(0, CHUNK // 8, lambda turn, carry: (pick(base, turn), carry)[1], 0)

    pick_chunk(0)

    for step in range(1, LAT):
        peer = lax.rem(lat + step, LAT)
        part = fields.at[pl.ds(2, 2), here_rows, pl.ds(0, COLS)]
        pltpu.make_async_remote_copy(
            src_ref=part,
            dst_ref=part,
            send_sem=lat_sems.at[0],
            recv_sem=lat_sems.at[1],
            device_id=(peer, lon),
            device_id_type=MESH,
        ).start()
    send_west = pltpu.make_async_remote_copy(
        src_ref=own_west,
        dst_ref=cols_east,
        send_sem=col_sems.at[0],
        recv_sem=col_sems.at[1],
        device_id=(lat, west),
        device_id_type=MESH,
    )
    send_east = pltpu.make_async_remote_copy(
        src_ref=own_east,
        dst_ref=cols_west,
        send_sem=col_sems.at[2],
        recv_sem=col_sems.at[3],
        device_id=(lat, east),
        device_id_type=MESH,
    )
    send_west.start()
    send_east.start()

    def north_copy(rows):
        return pltpu.make_async_remote_copy(
            src_ref=going_north.at[rows],
            dst_ref=from_south.at[rows],
            send_sem=row_sems.at[0],
            recv_sem=row_sems.at[1],
            device_id=(lat + 1, lon),
            device_id_type=MESH,
        )

    def south_copy(rows):
        return pltpu.make_async_remote_copy(
            src_ref=going_south.at[rows],
            dst_ref=from_north.at[rows],
            send_sem=row_sems.at[2],
            recv_sem=row_sems.at[3],
            device_id=(lat - 1, lon),
            device_id_type=MESH,
        )

    def send_chunk(number):
        rows = pl.ds(pl.multiple_of(number * CHUNK, CHUNK), CHUNK)

        @pl.when(lat < LAT - 1)
        def _():
            north_copy(rows).start()

        @pl.when(lat > 0)
        def _():
            south_copy(rows).start()

    def forward(number, carry):
        pick_chunk(number)
        send_chunk(number - 1)
        return carry

    lax.fori_loop(1, cap // CHUNK, forward, 0)

    @pl.when(lat == 0)
    def _():
        from_south[...] = jnp.zeros(from_south.shape, f32)

    @pl.when(lat == LAT - 1)
    def _():
        from_north[...] = jnp.zeros(from_north.shape, f32)

    send_chunk(cap // CHUNK - 1)

    got = pl.ds(0, DEV - 1)
    pltpu.make_async_copy(inbox.at[got], inbox.at[got], box_sems.at[1]).wait()
    turned[...] = inbox[...].T

    def place(number, carry):
        base = pl.multiple_of(number * 8, 8)
        misfits = turned[pl.ds(base, 8), :]
        weights = turned[pl.ds(base + 32, 8), :]
        cell = turned[pl.ds(base + 64, 8), :].astype(i32)
        cell_row = lax.shift_right_logical(cell, 8)
        cell_col = lax.bitwise_and(cell, 255)
        rows8 = lax.broadcasted_iota(i32, (8, LANES), 0)
        cols = lax.broadcasted_iota(i32, (COLS, LANES), 0)
        spots, sent = [], []
        for s in range(8):
            spots.append(jnp.where(cols == cell_col[s : s + 1, :], 1.0, 0.0).astype(bf16))
            at_row = rows8 == cell_row[s : s + 1, :]
            sent.append(
                jnp.concatenate(
                    [
                        jnp.where(at_row, misfits[s : s + 1, :], 0.0),
                        jnp.where(at_row, weights[s : s + 1, :], 0.0),
                    ],
                    axis=0,
                )
            )
        spots = jnp.concatenate(spots, axis=1)
        sent = jnp.concatenate(sent, axis=1)
        total = jnp.zeros((16, COLS), f32)
        for piece in thirds(sent):
            total = total + lax.dot_general(
                piece, spots, NT, preferred_element_type=f32
            )
        fields[0, pl.ds(base, 8), 0:COLS] = total[0:8, :]
        fields[1, pl.ds(base, 8), 0:COLS] = total[8:16, :]
        return carry

    lax.fori_loop(0, LAT, place, 0)

    three = fields.at[pl.ds(2, 2), pl.ds(0, NROW - ROWS), pl.ds(0, COLS)]
    pltpu.make_async_copy(three, three, lat_sems.at[1]).wait()
    pltpu.make_async_copy(three, three, lat_sems.at[0]).wait()
    height = fields[2, :, 0:COLS]
    ocean = fields[3, :, 0:COLS]
    weight = fields[1, :, 0:COLS] * ocean
    fields[0, :, 0:COLS] = (fields[0, :, 0:COLS] - height * fields[1, :, 0:COLS]) * ocean
    fields[1, :, 0:COLS] = weight

    rim_west = pltpu.make_async_remote_copy(
        src_ref=fields.at[pl.ds(0, 4), pl.ds(0, NROW), pl.ds(0, LANES)],
        dst_ref=near_east,
        send_sem=rim_sems.at[0],
        recv_sem=rim_sems.at[1],
        device_id=(lat, west),
        device_id_type=MESH,
    )
    rim_east = pltpu.make_async_remote_copy(
        src_ref=fields.at[pl.ds(0, 4), pl.ds(0, NROW), pl.ds(LANES, LANES)],
        dst_ref=near_west,
        send_sem=rim_sems.at[2],
        recv_sem=rim_sems.at[3],
        device_id=(lat, east),
        device_id_type=MESH,
    )
    rim_west.start()
    rim_east.start()
    rim_west.wait()
    rim_east.wait()
    lane = lax.broadcasted_iota(i32, (NROW, LANES), 1)
    for number, filler in enumerate((0.0, 0.0, 1.0, 0.0)):
        fields[number, :, COLS:EXT] = jnp.where(
            lane < RIM,
            near_east[number],
            jnp.where(lane >= LANES - RIM, near_west[number], filler),
        )

    row = lax.broadcasted_iota(i32, (NROW, EXT), 0)

    def north_of(x):
        return jnp.where(row == NROW - 1, 0.0, pltpu.roll(x, NROW - 1, 0))

    def south_of(x):
        return jnp.where(row == 0, 0.0, pltpu.roll(x, 1, 0))

    def east_of(x):
        return pltpu.roll(x, EXT - 1, 1)

    def west_of(x):
        return pltpu.roll(x, 1, 1)

    ocean = fields[3]
    share = spread_rate * ocean
    keep = 1.0 - share * (
        north_of(ocean) + south_of(ocean) + east_of(ocean) + west_of(ocean)
    )

    def relax(x):
        return keep * x + share * (
            (north_of(x) + south_of(x)) + (east_of(x) + west_of(x))
        )

    def relax_both(_, pair):
        return relax(pair[0]), relax(pair[1])

    misfit, weight = lax.fori_loop(0, PASSES, relax_both, (fields[0], fields[1]))
    increment = ocean * misfit / (prior_weight + weight)
    factor = jnp.exp(2.0 * increment / fields[2]) * ocean
    edge = jnp.zeros((8, EXT), f32)
    for number, value in enumerate(
        (
            factor,
            factor * east_of(ocean),
            factor * west_of(ocean),
            factor * north_of(ocean),
            factor * south_of(ocean),
            increment,
        )
    ):
        padded[number, 0:8, :] = edge
        padded[number, pl.ds(8, NROW), :] = value
        padded[number, pl.ds(8 + NROW, 8), :] = edge
    own = pl.ds(pl.multiple_of(8 + lat * ROWS, ROWS), ROWS)
    for number in range(6):
        tables[number] = padded[number, own, 0:COLS]
    below = padded[3, pl.ds(7 + lat * ROWS, 1), 0:COLS]
    above = padded[4, pl.ds(16 + lat * ROWS, 1), 0:COLS]
    tables[6] = jnp.broadcast_to(below, (ROWS, COLS))
    tables[7] = jnp.broadcast_to(above, (ROWS, COLS))
    tables[8, :, 0:LANES] = jnp.broadcast_to(
        padded[1, own, EXT - 1 : EXT], (ROWS, LANES)
    )
    tables[8, :, LANES:COLS] = jnp.broadcast_to(
        padded[2, own, COLS : COLS + 1], (ROWS, LANES)
    )

    pltpu.make_async_copy(inbox.at[got], inbox.at[got], box_sems.at[0]).wait()
    send_west.wait()
    send_east.wait()

    @pl.when(lat < LAT - 1)
    def _():
        north_copy(pl.ds(0, cap)).wait_send()
        south = pltpu.make_async_copy(from_north, from_north, row_sems.at[3])
        south.wait()

    @pl.when(lat > 0)
    def _():
        south_copy(pl.ds(0, cap)).wait_send()
        north = pltpu.make_async_copy(from_south, from_south, row_sems.at[1])
        north.wait()


def exchange(cap, picks, spectrum, reports, sea):
    vmem = pl.BlockSpec(memory_space=pltpu.VMEM)
    return pl.pallas_call(
        functools.partial(exchange_kernel, cap),
        out_shape=(
            jax.ShapeDtypeStruct((9, ROWS, COLS), f32),
            jax.ShapeDtypeStruct((cap, COLS), f32),
            jax.ShapeDtypeStruct((cap, COLS), f32),
            jax.ShapeDtypeStruct((GROUPS, ROWS, LANES), f32),
            jax.ShapeDtypeStruct((GROUPS, ROWS, LANES), f32),
        ),
        in_specs=[
            pl.BlockSpec(memory_space=pltpu.SMEM),
            pl.BlockSpec(memory_space=pl.ANY),
            vmem,
            vmem,
        ],
        out_specs=(vmem,) * 5,
        scratch_shapes=[
            pltpu.VMEM((SPEC, ROWS, COLS), f32),
            pltpu.VMEM((LON, LANES), f32),
            pltpu.VMEM((DEV, LANES), f32),
            pltpu.VMEM((LANES, DEV), f32),
            pltpu.VMEM((4, NROW, EXT), f32),
            pltpu.VMEM((4, NROW, LANES), f32),
            pltpu.VMEM((4, NROW, LANES), f32),
            pltpu.VMEM((GROUPS, ROWS, LANES), f32),
            pltpu.VMEM((GROUPS, ROWS, LANES), f32),
            pltpu.VMEM((6, NROW + 16, EXT), f32),
            pltpu.VMEM((cap, COLS), f32),
            pltpu.VMEM((cap, COLS), f32),
            pltpu.SemaphoreType.DMA((GROUPS,)),
            pltpu.SemaphoreType.DMA((2,)),
            pltpu.SemaphoreType.DMA((2,)),
            pltpu.SemaphoreType.DMA((4,)),
            pltpu.SemaphoreType.DMA((4,)),
            pltpu.SemaphoreType.DMA((4,)),
        ],
        compiler_params=pltpu.CompilerParams(
            collective_id=0 if cap == CAP_HALF else 1,
            has_side_effects=True,
            vmem_limit_bytes=30 * 2**20,
        ),
        name=f"exchange_{cap}",
    )(picks, spectrum, reports, sea)


def update_kernel(
    courant,
    spectrum,
    tables,
    from_south,
    from_north,
    cols_west,
    cols_east,
    out,
    increment,
    beside,
    counts,
):
    step = pl.program_id(0)

    @pl.when(step == 0)
    def _():
        counts[0] = 0
        increment[...] = tables[5]
        for group in range(GROUPS):
            beside[0, group] = cols_west[group] * tables[8, :, 0:LANES]
            beside[1, group] = cols_east[group] * tables[8, :, LANES:COLS]

    lane = lax.broadcasted_iota(i32, (ROWS, LANES), 1)
    sub = lax.broadcasted_iota(i32, (ROWS, COLS), 0)
    plain = tables[0]

    def one(at, south_count):
        number = step * BLOCK + at
        east_speed = courant[0, number]
        north_speed = courant[1, number]
        back_x = east_speed < 0.0
        back_y = north_speed < 0.0
        x = back_x.astype(i32)
        y = back_y.astype(i32)
        cell = spectrum[at]
        group = lax.shift_right_logical(number, 7)
        at_lane = lax.bitwise_and(number, 127)

        flow = cell * tables[1 + x]
        shift = jnp.where(back_x, LANES - 1, 1)
        edge_lane = jnp.where(back_x, LANES - 1, 0)
        left = pltpu.roll(flow[:, 0:LANES], shift, 1)
        right = pltpu.roll(flow[:, LANES:COLS], shift, 1)
        rim = pltpu.roll(
            beside[x, group], lax.bitwise_and(edge_lane - at_lane + LANES, 127), 1
        )
        at_edge = lane == edge_lane
        new_left = jnp.where(at_edge, jnp.where(back_x, right, rim), left)
        new_right = jnp.where(at_edge, jnp.where(back_x, rim, left), right)
        came_x = jnp.concatenate([new_left, new_right], axis=1)
        gone_x = flow - came_x

        flow = cell * tables[3 + y]
        rolled = pltpu.roll(flow, jnp.where(back_y, ROWS - 1, 1), 0)
        north_count = number - south_count
        row = jnp.where(
            back_y,
            from_north[pl.ds(jnp.where(back_y, south_count, 0), 1), :],
            from_south[pl.ds(jnp.where(back_y, 0, north_count), 1), :],
        )
        edge_row = jnp.where(back_y, ROWS - 1, 0)
        came_y = jnp.where(sub == edge_row, row * tables[6 + y], rolled)
        gone_y = flow - came_y
        out[at] = (
            cell * plain - jnp.abs(east_speed) * gone_x - jnp.abs(north_speed) * gone_y
        )
        return south_count + y

    counts[0] = lax.fori_loop(0, BLOCK, one, counts[0], unroll=4)


def update(cap, courant, spectrum, tables, from_south, from_north, cols_west, cols_east):
    def whole(*shape):
        return pl.BlockSpec(shape, lambda i: (0,) * len(shape))

    return pl.pallas_call(
        update_kernel,
        grid=(SPEC // BLOCK,),
        out_shape=(
            jax.ShapeDtypeStruct((SPEC, ROWS, COLS), f32),
            jax.ShapeDtypeStruct((ROWS, COLS), f32),
        ),
        in_specs=[
            pl.BlockSpec(memory_space=pltpu.SMEM),
            pl.BlockSpec((BLOCK, ROWS, COLS), lambda i: (i, 0, 0)),
            whole(9, ROWS, COLS),
            whole(cap, COLS),
            whole(cap, COLS),
            whole(GROUPS, ROWS, LANES),
            whole(GROUPS, ROWS, LANES),
        ],
        out_specs=(
            pl.BlockSpec((BLOCK, ROWS, COLS), lambda i: (i, 0, 0)),
            whole(ROWS, COLS),
        ),
        scratch_shapes=[
            pltpu.VMEM((2, GROUPS, ROWS, LANES), f32),
            pltpu.SMEM((1,), i32),
        ],
        compiler_params=pltpu.CompilerParams(dimension_semantics=("arbitrary",)),
        name=f"update_{cap}",
    )(courant, spectrum, tables, from_south, from_north, cols_west, cols_east)


def body(spectrum, sea_mask, courant, obs_tile, obs_cell, obs_value, obs_error):
    weights = 1.0 / obs_error
    reports = jnp.stack(
        [
            obs_tile[:, 0].astype(f32),
            weights * obs_value,
            weights,
            obs_cell.astype(f32),
        ]
    )
    backward = (courant[1] < 0.0).astype(i32)
    number = jnp.arange(SPEC, dtype=i32)
    through = number[None, :] <= number[:, None]
    south_upto = jnp.sum(jnp.where(through, backward[None, :], 0), axis=1)
    upto = jnp.stack([number + 1 - south_upto, south_upto])
    fits = jnp.max(upto[:, -1]) <= CAP_HALF

    def run(cap):
        place = jnp.arange(cap, dtype=i32)
        picks = jnp.sum((upto[:, None, :] <= place[None, :, None]).astype(i32), axis=2)
        picks = jnp.minimum(picks, SPEC - 1)
        tables, south, north, cols_w, cols_e = exchange(
            cap, picks, spectrum, reports, sea_mask
        )
        return update(cap, courant, spectrum, tables, south, north, cols_w, cols_e)

    return lax.cond(fits, lambda: run(CAP_HALF), lambda: run(CAP_ALL))


def solution(mesh):
    return jax.shard_map(
        body,
        mesh=mesh,
        in_specs=(
            P(None, "lat", "lon"),
            P("lat", "lon"),
            P(),
            P(("lat", "lon"), None),
            P(("lat", "lon")),
            P(("lat", "lon")),
            P(("lat", "lon")),
        ),
        out_specs=(P(None, "lat", "lon"), P("lat", "lon")),
        check_vma=False,
    )
```

time: 247 us -> 104 us (0.42)
  Pallas kernels: 0 us -> 93.6 us
  local copies, waits for them, and re-layouts: 75.3 us -> 3.59 us
  other arithmetic: 71.8 us -> 4.81 us
  waiting for transfers between devices: 52.8 us -> 0 us
  starting transfers between devices: 44.3 us -> 0 us
    pallas_call x0 -> x2, Pallas kernels: none -> 93.6 us  [the longest x1 51.7 us: exchange(): pl.pallas_call(functools.partial(exchange_kernel, cap), out_shape=(jax.Sh...]
    mul x8 -> x1, other arithmetic: 48.1 us -> 0.7 us  [body(): weights * obs_value]
    ppermute x28 -> x0, waiting for transfers between devices: 44.5 us -> none  [the longest x12 40.1 us: with_halo_2(): lax.ppermute(tail, axis, [(i, (i + 1) % count) for i in range(count)])]
    ppermute x28 -> x0, starting transfers between devices: 37 us -> none  [the longest x12 20.7 us: with_halo_2(): lax.ppermute(head, axis, [((i + 1) % count, i) for i in range(count)])]
    unnamed x20 -> x0, local copies, waits for them, and re-layouts: 33.9 us -> none
    slice x19 -> x0, local copies, waits for them, and re-layouts: 18.1 us -> none  [the longest x2 16.7 us: with_halo(): last = lax.slice_in_dim(array, length - width, length, axis=dim)]
    unnamed x6 -> x0, other arithmetic: 12.3 us -> none
    scatter x1 -> x0, local copies, waits for them, and re-layouts: 11.5 us -> none  [body(): outbox = jnp.zeros((3, devices, slot_cap), jnp.float32).at[:, owners, slo...]
  transfers between devices with their start and end apart: 30 -> 0, of which waited for: 12 -> 0; matrix products, arithmetic and copies ran while one was open for 27% -> 0% of each run, Pallas kernels for 0% -> 0%
where the time goes in v1:
time: 104 us; the launch traced here: 103 us
  Pallas kernels  93.6 us (90%)
  other arithmetic  4.81 us (5%)
  local copies, waits for them, and re-layouts  3.59 us (3%)
  between operations  1.32 us (1%)
    pallas_call x1, Pallas kernels, exchange(): pl.pallas_call(functools.partial(exchange_kernel, cap), out_shape=(jax.Sh...  51.7 us
    pallas_call x1, Pallas kernels, update(): pl.pallas_call(update_kernel, grid=(SPEC // BLOCK,), out_shape=(jax.Shape...  42 us
    cond x12, local copies, waits for them, and re-layouts  3.59 us

profile of v1, /device:TPU:0, one launch (start us, length us, event | category | flops | bytes accessed | tf_op | source)
XLA Modules:
  0.0 103.4 jit_solution(10473050962357263225)
XLA Ops:
  0.6 0.7 convert_bitcast_fusion
  1.3 0.7 convert_element_type.30
  2.0 0.7 fusion.3
  2.7 0.7 fusion
  3.4 0.3 select_reduce_fusion
  3.8 0.7 fusion.2
  5.1 98.3 %conditional.1 = ((f32[1296,8,256]{2,1,0:T(8,128)}, f32[8,256]{1,0:T(8,128)})) conditional(s32[]{:T(128)} %convert_element_type.27, (s32[2,1296]{1,0:T(2,128)S(1)}, f32[1296,8,256]{2,1,0:T(8,128)}, f32[4,256]{1,0:T(4,128)S(1)}, s32[8,256]{1,0:T(8,128)}, f32[2,1296]{1,0:T(2,128)}) %tuple.13, (s32[2,1296]{1,0:T(2,128)S(1)}, f32[1296,8,256]{2,1,0:T(8,128)}, ...), branch_computations={%region_2.4_spmd, %region_4.6_spmd} | conditional | flops 10450944 | bytes 11749680 | solution.py:608
  5.2 0.0 copy-start.11
  5.2 1.0 convert_reduce_fusion.1
  6.2 51.7 %exchange_704.1 = (f32[9,8,256]{2,1,0:T(8,128)S(1)}, f32[704,256]{1,0:T(8,128)S(1)}, f32[704,256]{1,0:T(8,128)S(1)}, f32[11,8,128]{2,1,0:T(8,128)S(1)}, f32[11,8,128]{2,1,0:T(8,128)S(1)}) custom-call(s32[2,704]{1,0:T(2,128)S(1)} %broadcast_minimum_fusion.1.picks, f32[1296,8,256]{2,1,0:T(8,128)} %get-tuple-element.53.spectrum, ...), custom_call_target="tpu_custom_call" | custom-call | tf_op jit(solution)/shard_map/cond/branch_1_fun/exchange_704/pallas_call | solution.py:432
  57.9 0.0 copy-start.2
  57.9 0.8 copy-done.2
  58.7 0.0 copy-start.3
  58.7 0.9 copy-done.3
  59.6 0.0 copy-start.4
  59.6 0.6 copy-done.4
  60.2 0.0 copy-start.6
  60.2 0.6 copy-done.6
  60.9 0.0 copy-start.7
  60.9 0.6 copy-done.7
  61.5 0.0 copy-done.11
  61.5 42.0 %update_704.1 = (f32[1296,8,256]{2,1,0:T(8,128)}, f32[8,256]{1,0:T(8,128)}) custom-call(f32[2,1296]{1,0:T(2,128)S(1)} %copy-done.11, f32[1296,8,256]{2,1,0:T(8,128)} %get-tuple-element.53.spectrum, f32[9,8,256]{2,1,0:T(8,128)} %copy-done.4, f32[704,256]{1,0:T(8,128)} %copy-done.2, f32[704,256]{1,0:T(8,128)} %copy-done.3, f32[11,8,128]{2,1,0:T(8,128)} %copy-done.6, ...), custom_call_target="tpu_custom_call" | custom-call | tf_op jit(solution)/shard_map/cond/branch_1_fun/update_704/pallas_call | solution.py:553
  (5 shorter events, 0.1 us)
Async XLA Ops:
  5.2 56.3 %copy-start.11 = (f32[2,1296]{1,0:T(2,128)S(1)}, f32[2,1296]{1,0:T(2,128)}, u32[]{:S(2)}) copy-start(f32[2,1296]{1,0:T(2,128)} %get-tuple-element.30.courant) | copy-start | bytes 31108 | tf_op jit(solution)/shard_map/cond
  57.9 0.9 copy-start.2
  58.7 0.9 copy-start.3
  59.6 0.6 copy-start.4
  60.2 0.6 copy-start.6
  60.9 0.6 copy-start.7

commit v2 on v1

v2 whole, which is shorter than its diff:
```python
import functools

import jax
import jax.numpy as jnp
from jax import lax
from jax.experimental import pallas as pl
from jax.experimental.pallas import tpu as pltpu
from jax.sharding import PartitionSpec as P

SPEC = 1296
ROWS = 8
COLS = 256
LAT = 4
LON = 32
DEV = LAT * LON
NROW = LAT * ROWS
PASSES = 8
LANES = 128
GROUP = 72
GROUPS = SPEC // GROUP
CELLS = SPEC * 16
LOADS = 6
MEMBERS = 72
EXT = 384
RIM = 9
CHUNK = 64
CAP_HALF = 704
CAP_ALL = 1344

spread_rate = 0.2
prior_weight = 4.0

f32 = jnp.float32
i32 = jnp.int32
bf16 = jnp.bfloat16
MESH = pl.DeviceIdType.MESH
LOGICAL = pl.DeviceIdType.LOGICAL
NT = (((1,), (1,)), ((), ()))
NN = (((1,), (0,)), ((), ()))


def thirds(x):
    high = x.astype(bf16)
    rest = x - high.astype(f32)
    mid = rest.astype(bf16)
    low = (rest - mid.astype(f32)).astype(bf16)
    return high, mid, low


def exchange_kernel(
    cap,
    spectrum,
    courant,
    by_group,
    obs_tile,
    obs_cell,
    obs_value,
    obs_error,
    sea,
    cells,
    tables,
    rows,
    cols_west,
    cols_east,
    plan,
    speeds,
    own_courant,
    own_groups,
    own_tile,
    own_cell,
    own_value,
    own_error,
    own_sea,
    outbox,
    inbox,
    turned,
    fields,
    near_west,
    near_east,
    own_edge,
    padded,
    going_north,
    going_south,
    listed,
    picks,
    load_sems,
    small_sems,
    list_sem,
    box_sems,
    lat_sems,
    col_sems,
    rim_sems,
    row_sems,
):
    lat = lax.axis_index("lat")
    lon = lax.axis_index("lon")
    me = lat * LON + lon
    west = lax.rem(lon + LON - 1, LON)
    east = lax.rem(lon + 1, LON)
    chunks = cap // CHUNK

    small = [
        pltpu.make_async_copy(source, target, small_sems.at[number])
        for number, (source, target) in enumerate(
            (
                (obs_tile, own_tile),
                (obs_error, own_error),
                (obs_value, own_value),
                (obs_cell, own_cell),
                (courant, own_courant),
                (by_group, own_groups),
                (by_group, speeds),
                (sea, own_sea),
            )
        )
    ]
    for copy in small:
        copy.start()
    size = CELLS // LOADS
    loads = [
        pltpu.make_async_copy(
            spectrum.at[pl.ds(part * size, size)],
            cells.at[pl.ds(8 + part * size, size)],
            load_sems.at[part],
        )
        for part in range(LOADS)
    ]
    for copy in loads:
        copy.start()

    barrier = pltpu.get_barrier_semaphore()

    def greet(turn, carry):
        for u in range(7):
            pl.semaphore_signal(
                barrier,
                inc=1,
                device_id=lax.rem(me + (turn * 7 + u + 1), DEV),
                device_id_type=LOGICAL,
            )
        return carry

    lax.fori_loop(0, 18, greet, 0)
    pl.semaphore_signal(
        barrier,
        inc=1,
        device_id=lax.rem(me + DEV - 1, DEV),
        device_id_type=LOGICAL,
    )

    for copy in small[0:4]:
        copy.wait()
    owner = own_tile[...]
    owner_lat = lax.shift_right_logical(owner, 5)
    owner_lon = lax.bitwise_and(owner, 31)
    tiles = lax.broadcasted_iota(i32, (DEV, 256), 0)
    hit = jnp.where(tiles == owner, 1.0, 0.0)
    before = jnp.where(
        lax.broadcasted_iota(i32, (256, 256), 0)
        < lax.broadcasted_iota(i32, (256, 256), 1),
        1.0,
        0.0,
    )
    earlier = lax.dot_general(
        hit.astype(bf16), before.astype(bf16), NN, preferred_element_type=f32
    )
    rank = jnp.sum(hit * earlier, axis=0, keepdims=True).astype(i32)
    slot = owner_lat * 8 + rank
    slots = lax.broadcasted_iota(i32, (32, 256), 0)
    in_slot = slots == slot
    to_lon = jnp.where(slots == owner_lon, 1.0, 0.0).astype(bf16)
    zero = jnp.zeros((32, 256), f32)
    weights = 1.0 / own_error[...]
    spread = jnp.concatenate(
        [
            jnp.where(in_slot, value, zero)
            for value in (weights * own_value[...], weights, own_cell[...].astype(f32))
        ]
        + [zero],
        axis=0,
    )
    packed = jnp.zeros((LON, LANES), f32)
    for piece in thirds(spread):
        packed = packed + lax.dot_general(
            to_lon, piece, NT, preferred_element_type=f32
        )
    outbox[...] = packed

    for copy in small[4:8]:
        copy.wait()
    number = lax.broadcasted_iota(i32, (16, LANES), 0) * LANES + lax.broadcasted_iota(
        i32, (16, LANES), 1
    )
    speed = jnp.concatenate(
        [own_courant[1:2, t * LANES : (t + 1) * LANES] for t in range(SPEC // LANES)]
        + [
            jnp.concatenate(
                [
                    own_courant[1:2, SPEC // LANES * LANES : SPEC],
                    jnp.zeros((1, LANES - SPEC % LANES), f32),
                ],
                axis=1,
            )
        ]
        + [jnp.zeros((15 - SPEC // LANES, LANES), f32)],
        axis=0,
    )
    backward = jnp.where(speed < 0.0, 1.0, 0.0).astype(bf16)
    upper = jnp.where(
        lax.broadcasted_iota(i32, (LANES, LANES), 0)
        <= lax.broadcasted_iota(i32, (LANES, LANES), 1),
        1.0,
        0.0,
    ).astype(bf16)
    within = lax.dot_general(backward, upper, NN, preferred_element_type=f32)
    whole = lax.dot_general(
        backward, jnp.ones((LANES, LANES), bf16), NN, preferred_element_type=f32
    )
    lower = jnp.where(
        lax.broadcasted_iota(i32, (16, 16), 1) < lax.broadcasted_iota(i32, (16, 16), 0),
        1.0,
        0.0,
    ).astype(bf16)
    south_upto = within + lax.dot_general(
        lower, whole.astype(bf16), NN, preferred_element_type=f32
    )
    beyond = number >= SPEC
    far = 4.0 * SPEC
    upto = (
        jnp.where(beyond, far, (number + 1).astype(f32) - south_upto),
        jnp.where(beyond, far, south_upto),
    )
    ones = jnp.ones((8, LANES), bf16)

    def enlist(turn, carry):
        place = (
            turn * LANES + lax.broadcasted_iota(i32, (LANES, LANES), 0)
        ).astype(f32)
        for side in range(2):
            count = jnp.zeros((LANES, LANES), f32)
            for t in range(SPEC // LANES + 1):
                count = count + jnp.where(upto[side][t : t + 1, :] <= place, 1.0, 0.0)
            total = lax.dot_general(
                ones, count.astype(bf16), NT, preferred_element_type=f32
            )
            listed[side, pl.ds(turn, 1), :] = jnp.maximum(
                jnp.minimum(total[0:1, :].astype(i32), SPEC - 1), 0
            )
        return carry

    lax.fori_loop(0, listed.shape[1], enlist, 0)
    to_scalars = pltpu.make_async_copy(listed, picks, list_sem)
    to_scalars.start()

    to_east = own_groups[0:GROUPS, :] < 0.0
    to_north = own_groups[GROUPS : 2 * GROUPS, :] < 0.0
    shape = (GROUPS, GROUP)
    group = lax.broadcasted_iota(i32, shape, 0)
    member = lax.broadcasted_iota(i32, shape, 1)
    number = group * GROUP + member
    backward = jnp.where(to_north, 1.0, 0.0).astype(bf16)
    upper = jnp.where(
        lax.broadcasted_iota(i32, (GROUP, GROUP), 0)
        < lax.broadcasted_iota(i32, (GROUP, GROUP), 1),
        1.0,
        0.0,
    ).astype(bf16)
    whole = lax.dot_general(
        backward, jnp.ones((GROUP, GROUP), bf16), NN, preferred_element_type=f32
    )
    lower = jnp.where(
        lax.broadcasted_iota(i32, (GROUPS, GROUPS), 1)
        < lax.broadcasted_iota(i32, (GROUPS, GROUPS), 0),
        1.0,
        0.0,
    ).astype(bf16)
    south = (
        lax.dot_general(backward, upper, NN, preferred_element_type=f32)
        + lax.dot_general(lower, whole.astype(bf16), NN, preferred_element_type=f32)
    ).astype(i32)
    plan[0] = jnp.where(to_east, LANES - 1, 1)
    plan[1] = jnp.where(
        to_east, LANES - 1 - member, jnp.where(member == 0, 0, LANES - member)
    )
    plan[2] = 8 + 16 * number + jnp.where(to_north, 1, -1)
    plan[3] = 2 * jnp.where(to_north, cap + south, number - south)

    def pick_chunk(number):
        def pick(turn, carry):
            for u in range(8):
                at = number * CHUNK + turn * 8 + u
                line = lax.div(number, 2)
                spot = lax.rem(number, 2) * CHUNK + turn * 8 + u
                first = 8 + 16 * picks[0, line, spot]
                going_north[pl.ds(2 * at, 1), :] = cells[pl.ds(first + 7, 1), :]
                going_north[pl.ds(2 * at + 1, 1), :] = cells[pl.ds(first + 15, 1), :]
                first = 8 + 16 * picks[1, line, spot]
                going_south[pl.ds(2 * at, 1), :] = cells[pl.ds(first, 1), :]
                going_south[pl.ds(2 * at + 1, 1), :] = cells[pl.ds(first + 8, 1), :]
            return carry

        lax.fori_loop(0, CHUNK // 8, pick, 0)

    def north_copy(first, count):
        return pltpu.make_async_remote_copy(
            src_ref=going_north.at[pl.ds(first, count)],
            dst_ref=rows.at[pl.ds(first, count)],
            send_sem=row_sems.at[0],
            recv_sem=row_sems.at[1],
            device_id=(lat + 1, lon),
            device_id_type=MESH,
        )

    def south_copy(first, count):
        return pltpu.make_async_remote_copy(
            src_ref=going_south.at[pl.ds(first, count)],
            dst_ref=rows.at[pl.ds(2 * cap + first, count)],
            send_sem=row_sems.at[2],
            recv_sem=row_sems.at[3],
            device_id=(lat - 1, lon),
            device_id_type=MESH,
        )

    def send_chunk(number):
        first = pl.multiple_of(number * (2 * CHUNK), 2 * CHUNK)

        @pl.when(lat < LAT - 1)
        def _():
            north_copy(first, 2 * CHUNK).start()

        @pl.when(lat > 0)
        def _():
            south_copy(first, 2 * CHUNK).start()

    pl.semaphore_wait(barrier, DEV - 1)
    def post(turn, carry):
        for u in range(7):
            peer = lax.rem(me + (turn * 7 + u + 1), DEV)
            post_to(peer)
        return carry

    def post_to(peer):
        pltpu.make_async_remote_copy(
            src_ref=outbox.at[pl.ds(lax.rem(peer, LON), 1)],
            dst_ref=inbox.at[pl.ds(me, 1)],
            send_sem=box_sems.at[0],
            recv_sem=box_sems.at[1],
            device_id=peer,
            device_id_type=LOGICAL,
        ).start()

    lax.fori_loop(0, 18, post, 0)
    post_to(lax.rem(me + DEV - 1, DEV))
    inbox[pl.ds(me, 1), :] = outbox[pl.ds(lon, 1), :]

    for copy in loads:
        copy.wait()
    to_scalars.wait()
    pick_chunk(0)
    pick_chunk(1)
    send_chunk(0)
    send_chunk(1)

    lane = lax.broadcasted_iota(i32, (ROWS, LANES), 1)
    blank = jnp.zeros((ROWS, LANES), f32)

    def gather(pair, sums):
        sums = list(sums)
        for half in range(2):
            group = 2 * pair + half
            edge = blank
            for u in range(GROUP):
                at = 8 + (group * GROUP + u) * 16
                left = cells[pl.ds(pl.multiple_of(at, 8), ROWS), :]
                right = cells[pl.ds(pl.multiple_of(at + 8, 8), ROWS), :]
                k = 2 * (u % 4)
                sums[k] = sums[k] + left
                sums[k + 1] = sums[k + 1] + right
                speed = speeds[group, u]
                taken = jnp.where(jnp.full((ROWS, LANES), speed) < 0.0, left, right)
                turn = jnp.where(speed < 0.0, u, u + 1)
                edge = jnp.where(lane == u, pltpu.roll(taken, turn, 1), edge)
            own_edge[group] = edge
        return tuple(sums)

    sums = lax.fori_loop(0, GROUPS // 2, gather, tuple(blank for _ in range(8)))
    left = (sums[0] + sums[2]) + (sums[4] + sums[6])
    right = (sums[1] + sums[3]) + (sums[5] + sums[7])
    here_rows = pl.ds(pl.multiple_of(lat * ROWS, ROWS), ROWS)
    fields[2, here_rows, 0:LANES] = 4.0 * jnp.sqrt(left / SPEC)
    fields[2, here_rows, LANES:COLS] = 4.0 * jnp.sqrt(right / SPEC)
    fields[3, here_rows, 0:COLS] = own_sea[...].astype(f32)

    for step in range(1, LAT):
        peer = lax.rem(lat + step, LAT)
        part = fields.at[pl.ds(2, 2), here_rows, pl.ds(0, COLS)]
        pltpu.make_async_remote_copy(
            src_ref=part,
            dst_ref=part,
            send_sem=lat_sems.at[0],
            recv_sem=lat_sems.at[1],
            device_id=(peer, lon),
            device_id_type=MESH,
        ).start()

    send_west = pltpu.make_async_remote_copy(
        src_ref=own_edge,
        dst_ref=cols_east,
        send_sem=col_sems.at[0],
        recv_sem=col_sems.at[1],
        device_id=(lat, west),
        device_id_type=MESH,
    )
    send_east = pltpu.make_async_remote_copy(
        src_ref=own_edge,
        dst_ref=cols_west,
        send_sem=col_sems.at[2],
        recv_sem=col_sems.at[3],
        device_id=(lat, east),
        device_id_type=MESH,
    )
    send_west.start()
    send_east.start()

    pick_chunk(2)

    def forward(number, carry):
        pick_chunk(number)
        send_chunk(number - 1)
        return carry

    lax.fori_loop(3, chunks, forward, 0)

    @pl.when(lat == 0)
    def _():
        rows[0 : 2 * cap, :] = jnp.zeros((2 * cap, LANES), f32)

    @pl.when(lat == LAT - 1)
    def _():
        rows[2 * cap : 4 * cap, :] = jnp.zeros((2 * cap, LANES), f32)

    send_chunk(chunks - 1)

    got = pl.ds(0, DEV - 1)
    pltpu.make_async_copy(inbox.at[got], inbox.at[got], box_sems.at[1]).wait()
    turned[...] = inbox[...].T

    def place(number, carry):
        base = pl.multiple_of(number * 8, 8)
        misfits = turned[pl.ds(base, 8), :]
        weights = turned[pl.ds(base + 32, 8), :]
        cell = turned[pl.ds(base + 64, 8), :].astype(i32)
        cell_row = lax.shift_right_logical(cell, 8)
        cell_col = lax.bitwise_and(cell, 255)
        rows8 = lax.broadcasted_iota(i32, (8, LANES), 0)
        cols = lax.broadcasted_iota(i32, (COLS, LANES), 0)
        spots, sent = [], []
        for s in range(8):
            spots.append(jnp.where(cols == cell_col[s : s + 1, :], 1.0, 0.0).astype(bf16))
            at_row = rows8 == cell_row[s : s + 1, :]
            sent.append(
                jnp.concatenate(
                    [
                        jnp.where(at_row, misfits[s : s + 1, :], 0.0),
                        jnp.where(at_row, weights[s : s + 1, :], 0.0),
                    ],
                    axis=0,
                )
            )
        spots = jnp.concatenate(spots, axis=1)
        sent = jnp.concatenate(sent, axis=1)
        total = lax.dot_general(
            jnp.concatenate(thirds(sent), axis=0), spots, NT, preferred_element_type=f32
        )
        total = total[0:16, :] + total[16:32, :] + total[32:48, :]
        fields[0, pl.ds(base, 8), 0:COLS] = total[0:8, :]
        fields[1, pl.ds(base, 8), 0:COLS] = total[8:16, :]
        return carry

    lax.fori_loop(0, LAT, place, 0)

    three = fields.at[pl.ds(2, 2), pl.ds(0, NROW - ROWS), pl.ds(0, COLS)]
    pltpu.make_async_copy(three, three, lat_sems.at[1]).wait()
    pltpu.make_async_copy(three, three, lat_sems.at[0]).wait()
    height = fields[2, :, 0:COLS]
    ocean = fields[3, :, 0:COLS]
    weight = fields[1, :, 0:COLS] * ocean
    fields[0, :, 0:COLS] = (fields[0, :, 0:COLS] - height * fields[1, :, 0:COLS]) * ocean
    fields[1, :, 0:COLS] = weight

    rim_west = pltpu.make_async_remote_copy(
        src_ref=fields.at[pl.ds(0, 4), pl.ds(0, NROW), pl.ds(0, LANES)],
        dst_ref=near_east,
        send_sem=rim_sems.at[0],
        recv_sem=rim_sems.at[1],
        device_id=(lat, west),
        device_id_type=MESH,
    )
    rim_east = pltpu.make_async_remote_copy(
        src_ref=fields.at[pl.ds(0, 4), pl.ds(0, NROW), pl.ds(LANES, LANES)],
        dst_ref=near_west,
        send_sem=rim_sems.at[2],
        recv_sem=rim_sems.at[3],
        device_id=(lat, east),
        device_id_type=MESH,
    )
    rim_west.start()
    rim_east.start()
    rim_west.wait()
    rim_east.wait()
    lane = lax.broadcasted_iota(i32, (NROW, LANES), 1)
    for number, filler in enumerate((0.0, 0.0, 1.0, 0.0)):
        fields[number, :, COLS:EXT] = jnp.where(
            lane < RIM,
            near_east[number],
            jnp.where(lane >= LANES - RIM, near_west[number], filler),
        )

    row = lax.broadcasted_iota(i32, (NROW, EXT), 0)

    def north_of(x):
        return jnp.where(row == NROW - 1, 0.0, pltpu.roll(x, NROW - 1, 0))

    def south_of(x):
        return jnp.where(row == 0, 0.0, pltpu.roll(x, 1, 0))

    def east_of(x):
        return pltpu.roll(x, EXT - 1, 1)

    def west_of(x):
        return pltpu.roll(x, 1, 1)

    ocean = fields[3]
    share = spread_rate * ocean
    keep = 1.0 - share * (
        north_of(ocean) + south_of(ocean) + east_of(ocean) + west_of(ocean)
    )

    def relax(x):
        return keep * x + share * (
            (north_of(x) + south_of(x)) + (east_of(x) + west_of(x))
        )

    def relax_both(_, pair):
        return relax(pair[0]), relax(pair[1])

    misfit, weight = lax.fori_loop(0, PASSES, relax_both, (fields[0], fields[1]))
    increment = ocean * misfit / (prior_weight + weight)
    factor = jnp.exp(2.0 * increment / fields[2]) * ocean
    going_up = factor * north_of(ocean)
    going_down = factor * south_of(ocean)
    for number, value in enumerate(
        (
            factor,
            factor * east_of(ocean),
            factor * west_of(ocean),
            going_up,
            going_down,
            south_of(going_up),
            north_of(going_down),
            increment,
        )
    ):
        padded[number] = value
    own = here_rows
    for number in range(8):
        tables[16 * number : 16 * number + 8, :] = padded[number, own, 0:LANES]
        tables[16 * number + 8 : 16 * number + 16, :] = padded[
            number, own, LANES:COLS
        ]
    tables[128:136, :] = jnp.broadcast_to(
        padded[1, own, EXT - 1 : EXT], (ROWS, LANES)
    )
    tables[136:144, :] = jnp.broadcast_to(
        padded[2, own, COLS : COLS + 1], (ROWS, LANES)
    )

    pltpu.make_async_copy(inbox.at[got], inbox.at[got], box_sems.at[0]).wait()
    send_west.wait()
    send_east.wait()

    @pl.when(lat < LAT - 1)
    def _():
        north_copy(0, 2 * cap).wait_send()
        part = rows.at[pl.ds(2 * cap, 2 * cap)]
        pltpu.make_async_copy(part, part, row_sems.at[3]).wait()

    @pl.when(lat > 0)
    def _():
        south_copy(0, 2 * cap).wait_send()
        part = rows.at[pl.ds(0, 2 * cap)]
        pltpu.make_async_copy(part, part, row_sems.at[1]).wait()


def exchange(cap, spectrum, courant, by_group, *observed):
    vmem = pl.BlockSpec(memory_space=pltpu.VMEM)
    lists = -(-cap // LANES)
    return pl.pallas_call(
        functools.partial(exchange_kernel, cap),
        out_shape=(
            jax.ShapeDtypeStruct((CELLS + 16, LANES), f32),
            jax.ShapeDtypeStruct((144, LANES), f32),
            jax.ShapeDtypeStruct((4 * cap, LANES), f32),
            jax.ShapeDtypeStruct((GROUPS, ROWS, LANES), f32),
            jax.ShapeDtypeStruct((GROUPS, ROWS, LANES), f32),
            jax.ShapeDtypeStruct((4, GROUPS, GROUP), i32),
        ),
        in_specs=[pl.BlockSpec(memory_space=pl.ANY)] * 8,
        out_specs=(vmem,) * 6,
        scratch_shapes=[
            pltpu.SMEM((2 * GROUPS, GROUP), f32),
            pltpu.VMEM((2, SPEC), f32),
            pltpu.VMEM((2 * GROUPS, GROUP), f32),
            pltpu.VMEM((1, 256), i32),
            pltpu.VMEM((1, 256), i32),
            pltpu.VMEM((1, 256), f32),
            pltpu.VMEM((1, 256), f32),
            pltpu.VMEM((ROWS, COLS), i32),
            pltpu.VMEM((LON, LANES), f32),
            pltpu.VMEM((DEV, LANES), f32),
            pltpu.VMEM((LANES, DEV), f32),
            pltpu.VMEM((4, NROW, EXT), f32),
            pltpu.VMEM((4, NROW, LANES), f32),
            pltpu.VMEM((4, NROW, LANES), f32),
            pltpu.VMEM((GROUPS, ROWS, LANES), f32),
            pltpu.VMEM((8, NROW, EXT), f32),
            pltpu.VMEM((2 * cap, LANES), f32),
            pltpu.VMEM((2 * cap, LANES), f32),
            pltpu.VMEM((2, lists, LANES), i32),
            pltpu.SMEM((2, lists, LANES), i32),
            pltpu.SemaphoreType.DMA((LOADS,)),
            pltpu.SemaphoreType.DMA((8,)),
            pltpu.SemaphoreType.DMA,
            pltpu.SemaphoreType.DMA((2,)),
            pltpu.SemaphoreType.DMA((2,)),
            pltpu.SemaphoreType.DMA((4,)),
            pltpu.SemaphoreType.DMA((4,)),
            pltpu.SemaphoreType.DMA((4,)),
        ],
        compiler_params=pltpu.CompilerParams(
            collective_id=0 if cap == CAP_HALF else 1,
            has_side_effects=True,
            vmem_limit_bytes=30 * 2**20,
        ),
        name=f"exchange_{cap}",
    )(spectrum, courant, by_group, *observed)


def update_kernel(
    by_group,
    cells,
    tables,
    rows,
    cols_west,
    cols_east,
    plan,
    out,
    increment,
    steps,
    sem,
):
    step = pl.program_id(0)

    @pl.when(step == 0)
    def _():
        copy = pltpu.make_async_copy(plan, steps, sem)
        copy.start()
        increment[:, 0:LANES] = tables[112:120, :]
        increment[:, LANES:COLS] = tables[120:128, :]
        copy.wait()

    lane = lax.broadcasted_iota(i32, (ROWS, LANES), 1)
    sub = lax.broadcasted_iota(i32, (ROWS, LANES), 0)
    plain = tables[0:8, :], tables[8:16, :]

    def eight(ref, first):
        return ref[pl.ds(pl.multiple_of(first, 8), 8), :]

    def some(part, carry):
        for u in range(MEMBERS):
            one(part * MEMBERS + u)
        return carry

    def one(u):
        at = 8 + (step * GROUP + u) * 16
        cell = eight(cells, at), eight(cells, at + 8)
        speed = jnp.full((ROWS, LANES), by_group[step, u])
        back = speed < 0.0
        flow = [
            cell[half]
            * jnp.where(
                back,
                tables[32 + 8 * half : 40 + 8 * half, :],
                tables[16 + 8 * half : 24 + 8 * half, :],
            )
            for half in range(2)
        ]
        shift = steps[0, step, u]
        moved = pltpu.roll(flow[0], shift, 1), pltpu.roll(flow[1], shift, 1)
        rim = pltpu.roll(jnp.where(back, rims[1], rims[0]), steps[1, step, u], 1)
        at_edge = lane == jnp.where(back, LANES - 1, 0)
        came = (
            jnp.where(at_edge, jnp.where(back, moved[1], rim), moved[0]),
            jnp.where(at_edge, jnp.where(back, rim, moved[0]), moved[1]),
        )
        speed = jnp.abs(speed)

        slow = jnp.full((ROWS, LANES), by_group[GROUPS + step, u])
        down = slow < 0.0
        at_row = sub == jnp.where(down, ROWS - 1, 0)
        slow = jnp.abs(slow)
        near = steps[2, step, u]
        place = steps[3, step, u]
        for half in range(2):
            beyond = jnp.where(
                at_row,
                jnp.broadcast_to(rows[pl.ds(place + half, 1), :], (ROWS, LANES)),
                cells[pl.ds(near + 8 * half, 8), :],
            )
            first = 8 * half
            way = jnp.where(
                down, tables[64 + first : 72 + first, :], tables[48 + first : 56 + first, :]
            )
            way_in = jnp.where(
                down, tables[96 + first : 104 + first, :], tables[80 + first : 88 + first, :]
            )
            gone = cell[half] * way - beyond * way_in
            out[pl.ds(pl.multiple_of(u * 16 + first, 8), 8), :] = (
                cell[half] * plain[half]
                - speed * (flow[half] - came[half])
                - slow * gone
            )

    rims = cols_west[step] * tables[128:136, :], cols_east[step] * tables[136:144, :]
    lax.fori_loop(0, GROUP // MEMBERS, some, 0)


def update(cap, by_group, cells, tables, rows, cols_west, cols_east, plan):
    vmem = pl.BlockSpec(memory_space=pltpu.VMEM)
    return pl.pallas_call(
        update_kernel,
        grid=(GROUPS,),
        out_shape=(
            jax.ShapeDtypeStruct((CELLS, LANES), f32),
            jax.ShapeDtypeStruct((ROWS, COLS), f32),
        ),
        in_specs=[pl.BlockSpec(memory_space=pltpu.SMEM)] + [vmem] * 6,
        out_specs=(
            pl.BlockSpec((GROUP * 16, LANES), lambda i: (i, 0)),
            pl.BlockSpec((ROWS, COLS), lambda i: (0, 0)),
        ),
        scratch_shapes=[
            pltpu.SMEM((4, GROUPS, GROUP), i32),
            pltpu.SemaphoreType.DMA,
        ],
        compiler_params=pltpu.CompilerParams(
            dimension_semantics=("arbitrary",), vmem_limit_bytes=24 * 2**20
        ),
        name=f"update_{cap}",
    )(by_group, cells, tables, rows, cols_west, cols_east, plan)


def body(spectrum, sea_mask, courant, obs_tile, obs_cell, obs_value, obs_error):
    halves = spectrum.reshape(SPEC, ROWS, 2, LANES).transpose(0, 2, 1, 3)
    observed = (
        obs_tile.reshape(1, -1),
        obs_cell.reshape(1, -1),
        obs_value.reshape(1, -1),
        obs_error.reshape(1, -1),
        sea_mask,
    )
    by_group = courant.reshape(2 * GROUPS, GROUP)
    south = jnp.sum((courant[1] < 0.0).astype(i32))
    fits = jnp.maximum(south, SPEC - south) <= CAP_HALF

    def run(cap):
        sent = exchange(
            cap, halves.reshape(CELLS, LANES), courant, by_group, *observed
        )
        return update(cap, by_group, *sent)

    updated, increment = lax.cond(
        fits, lambda: run(CAP_HALF), lambda: run(CAP_ALL)
    )
    updated = updated.reshape(SPEC, 2, ROWS, LANES).transpose(0, 2, 1, 3)
    return updated.reshape(SPEC, ROWS, COLS), increment


def solution(mesh):
    return jax.shard_map(
        body,
        mesh=mesh,
        in_specs=(
            P(None, "lat", "lon"),
            P("lat", "lon"),
            P(),
            P(("lat", "lon"), None),
            P(("lat", "lon")),
            P(("lat", "lon")),
            P(("lat", "lon")),
        ),
        out_specs=(P(None, "lat", "lon"), P("lat", "lon")),
        check_vma=False,
    )
```

time: 104 us -> 49.8 us (0.48)
  Pallas kernels: 93.6 us -> 44.8 us
  other arithmetic: 4.81 us -> 1.36 us
  local copies, waits for them, and re-layouts: 3.59 us -> 0.79 us
    pallas_call x1, Pallas kernels: 42 us -> 14.8 us  [update(): pl.pallas_call(update_kernel, grid=(GROUPS,), out_shape=(jax.ShapeDtypeSt...]
    pallas_call x1, Pallas kernels: 51.7 us -> 29.9 us  [exchange(): pl.pallas_call(functools.partial(exchange_kernel, cap), out_shape=(jax.Sh...]
    cond x12 -> x0, local copies, waits for them, and re-layouts: 3.59 us -> none
    convert_element_type x2 -> x0, other arithmetic: 1.36 us -> none  [the longest x1 0.68 us: body(): obs_tile[:, 0].astype(f32)]
where the time goes in v2:
time: 49.8 us; the launch traced here: 48.9 us
  Pallas kernels  44.8 us (90%)
  between operations  1.94 us (4%)
  other arithmetic  1.36 us (3%)
  local copies, waits for them, and re-layouts  0.79 us (2%)
    pallas_call x1, Pallas kernels, exchange(): pl.pallas_call(functools.partial(exchange_kernel, cap), out_shape=(jax.Sh...  29.9 us
    pallas_call x1, Pallas kernels, update(): pl.pallas_call(update_kernel, grid=(GROUPS,), out_shape=(jax.ShapeDtypeSt...  14.8 us
    reduce_sum x1, other arithmetic, body(): south = jnp.sum((courant[1] < 0.0).astype(i32))  1.36 us

profile of v2, /device:TPU:0, one launch (start us, length us, event | category | flops | bytes accessed | tf_op | source)
XLA Modules:
  0.0 48.9 jit_solution(17574403847912659563)
XLA Ops:
  0.6 1.4 %fusion = s32[]{:T(128)} fusion(f32[2,1296]{1,0:T(2,128)} %param.11), kind=kLoop, calls=%fused_computation.1 | loop fusion | flops 3887 | bytes 5188 | tf_op jit(solution)/shard_map/reduce_sum | solution.py:773
  3.3 0.8 %reshape.38 = f32[36,72]{1,0:T(8,128)S(1)} reshape(f32[2,1296]{1,0:T(2,128)} %param.11) | data formatting | bytes 20736 | tf_op jit(solution)/shard_map/reshape | solution.py:772
  4.1 44.8 %conditional.1 = ((f32[20736,128]{1,0:T(8,128)}, f32[8,256]{1,0:T(8,128)})) conditional(s32[]{:T(128)} %convert_element_type.8, (f32[1296,2,8,128]{3,2,1,0:T(8,128)}, f32[2,1296]{1,0:T(2,128)}, f32[36,72]{1,0:T(8,128)S(1)}, s32[1,256]{1,0:T(1,128)}, s32[1,256]{1,0:T(1,128)}, /*index=5*/f32[1,256]{1,0:T(1,128)}, f32[1,256]{1,0:T(1,128)}, ...), branch_computations={%region_1.0_spmd, %region_2.0_spmd} | conditional | bytes 8 | solution.py:782
  4.1 29.9 %exchange_704.1 = (f32[20752,128]{1,0:T(8,128)S(1)}, f32[144,128]{1,0:T(8,128)S(1)}, f32[2816,128]{1,0:T(8,128)S(1)}, f32[18,8,128]{2,1,0:T(8,128)S(1)}, f32[18,...) custom-call(f32[20736,128]{1,0:T(8,128)} %bitcast.17, f32[2,1296]{1,0:T(2,128)} %get-tuple-element.48.courant, ...), custom_call_target="tpu_custom_call" | custom-call | tf_op jit(solution)/shard_map/cond/branch_1_fun/exchange_704/pallas_call | solution.py:598
  34.0 14.8 %update_704.1 = (f32[20736,128]{1,0:T(8,128)}, f32[8,256]{1,0:T(8,128)}) custom-call(f32[36,72]{1,0:T(8,128)S(1)} %get-tuple-element.46.by_group, f32[20752,128]{1,0:T(8,128)S(1)} %get-tuple-element.54.cells, f32[144,128]{1,0:T(8,128)S(1)} %get-tuple-element.55.tables, f32[2816,128]{1,0:T(8,128)S(1)} %get-tuple-element.56.rows, ...), custom_call_target="tpu_custom_call" | custom-call | tf_op jit(solution)/shard_map/cond/branch_1_fun/update_704/pallas_call | solution.py:740

commit v3 on v2

--- a/solution.py
+++ b/solution.py
@@ -20,7 +20,6 @@
 GROUPS = SPEC // GROUP
 CELLS = SPEC * 16
 LOADS = 6
-MEMBERS = 72
 EXT = 384
 RIM = 9
 CHUNK = 64
@@ -51,21 +50,25 @@
     cap,
     spectrum,
     courant,
-    by_group,
     obs_tile,
     obs_cell,
     obs_value,
     obs_error,
     sea,
+    partial,
+    rim_tables,
+    increments,
+    rows,
+    places,
+    own_groups,
     cells,
     tables,
-    rows,
     cols_west,
     cols_east,
     plan,
+    steps,
     speeds,
     own_courant,
-    own_groups,
     own_tile,
     own_cell,
     own_value,
@@ -108,8 +111,6 @@
                 (obs_value, own_value),
                 (obs_cell, own_cell),
                 (courant, own_courant),
-                (by_group, own_groups),
-                (by_group, speeds),
                 (sea, own_sea),
             )
         )
@@ -186,8 +187,13 @@
         )
     outbox[...] = packed
 
-    for copy in small[4:8]:
+    for copy in small[4:6]:
         copy.wait()
+    for group in range(GROUPS):
+        for way in range(2):
+            own_groups[way * GROUPS + group : way * GROUPS + group + 1, :] = own_courant[
+                way : way + 1, group * GROUP : (group + 1) * GROUP
+            ]
     number = lax.broadcasted_iota(i32, (16, LANES), 0) * LANES + lax.broadcasted_iota(
         i32, (16, LANES), 1
     )
@@ -283,7 +289,15 @@
         to_east, LANES - 1 - member, jnp.where(member == 0, 0, LANES - member)
     )
     plan[2] = 8 + 16 * number + jnp.where(to_north, 1, -1)
-    plan[3] = 2 * jnp.where(to_north, cap + south, number - south)
+    places[...] = 2 * jnp.where(to_north, cap + south, number - south)
+    scalars = [
+        pltpu.make_async_copy(plan, steps, small_sems.at[6]),
+        pltpu.make_async_copy(own_groups, speeds, small_sems.at[7]),
+    ]
+    for copy in scalars:
+        copy.start()
+    cells[0:8, :] = jnp.zeros((8, LANES), f32)
+    cells[8 + CELLS : 16 + CELLS, :] = jnp.zeros((8, LANES), f32)
 
     def pick_chunk(number):
         def pick(turn, carry):
@@ -356,6 +370,8 @@
     for copy in loads:
         copy.wait()
     to_scalars.wait()
+    for copy in scalars:
+        copy.wait()
     pick_chunk(0)
     pick_chunk(1)
     send_chunk(0)
@@ -563,21 +579,77 @@
     ):
         padded[number] = value
     own = here_rows
-    for number in range(8):
-        tables[16 * number : 16 * number + 8, :] = padded[number, own, 0:LANES]
-        tables[16 * number + 8 : 16 * number + 16, :] = padded[
-            number, own, LANES:COLS
-        ]
-    tables[128:136, :] = jnp.broadcast_to(
-        padded[1, own, EXT - 1 : EXT], (ROWS, LANES)
-    )
-    tables[136:144, :] = jnp.broadcast_to(
-        padded[2, own, COLS : COLS + 1], (ROWS, LANES)
-    )
-
-    pltpu.make_async_copy(inbox.at[got], inbox.at[got], box_sems.at[0]).wait()
+    sub = lax.broadcasted_iota(i32, (ROWS, LANES), 0)
+    for number in range(7):
+        for half in range(2):
+            value = padded[number, own, half * LANES : (half + 1) * LANES]
+            if number == 5:
+                rim_tables[8 * half : 8 * half + 8, :] = jnp.where(sub == 0, value, 0.0)
+                value = jnp.where(sub == 0, 0.0, value)
+            if number == 6:
+                outer = sub == ROWS - 1
+                rim_tables[16 + 8 * half : 24 + 8 * half, :] = jnp.where(
+                    outer, value, 0.0
+                )
+                value = jnp.where(outer, 0.0, value)
+            tables[16 * number + 8 * half : 16 * number + 8 * half + 8, :] = value
+    increments[...] = padded[7, own, 0:COLS]
+    beside = (
+        jnp.broadcast_to(padded[1, own, EXT - 1 : EXT], (ROWS, LANES)),
+        jnp.broadcast_to(padded[2, own, COLS : COLS + 1], (ROWS, LANES)),
+    )
+
     send_west.wait()
     send_east.wait()
+
+    def advance(step, carry):
+        rims = cols_west[step] * beside[0], cols_east[step] * beside[1]
+        for u in range(GROUP):
+            at = 8 + (step * GROUP + u) * 16
+            near = steps[2, step, u]
+            speed = jnp.full((ROWS, LANES), speeds[step, u])
+            back = speed < 0.0
+            cell, flow = [], []
+            for half in range(2):
+                first = 8 * half
+                cell.append(cells[pl.ds(pl.multiple_of(at + first, 8), 8), :])
+                way = jnp.where(
+                    back, tables[32 + first : 40 + first, :], tables[16 + first : 24 + first, :]
+                )
+                flow.append(cell[half] * way)
+            shift = steps[0, step, u]
+            moved = pltpu.roll(flow[0], shift, 1), pltpu.roll(flow[1], shift, 1)
+            rim = pltpu.roll(jnp.where(back, rims[1], rims[0]), steps[1, step, u], 1)
+            at_edge = lane == jnp.where(back, LANES - 1, 0)
+            came = (
+                jnp.where(at_edge, jnp.where(back, moved[1], rim), moved[0]),
+                jnp.where(at_edge, jnp.where(back, rim, moved[0]), moved[1]),
+            )
+            speed = jnp.abs(speed)
+            slow = jnp.full((ROWS, LANES), speeds[GROUPS + step, u])
+            down = slow < 0.0
+            slow = jnp.abs(slow)
+            for half in range(2):
+                first = 8 * half
+                way = jnp.where(
+                    down, tables[64 + first : 72 + first, :], tables[48 + first : 56 + first, :]
+                )
+                way_in = jnp.where(
+                    down, tables[96 + first : 104 + first, :], tables[80 + first : 88 + first, :]
+                )
+                gone = cell[half] * way - cells[pl.ds(near + first, 8), :] * way_in
+                to = pl.multiple_of((step * GROUP + u) * 16 + first, 8)
+                partial[pl.ds(to, 8), :] = (
+                    cell[half] * tables[first : first + 8, :]
+                    - speed * (flow[half] - came[half])
+                    - slow * gone
+                )
+        return carry
+
+    lane = lax.broadcasted_iota(i32, (ROWS, LANES), 1)
+    lax.fori_loop(0, GROUPS, advance, 0)
+
+    pltpu.make_async_copy(inbox.at[got], inbox.at[got], box_sems.at[0]).wait()
 
     @pl.when(lat < LAT - 1)
     def _():
@@ -592,25 +664,30 @@
         pltpu.make_async_copy(part, part, row_sems.at[1]).wait()
 
 
-def exchange(cap, spectrum, courant, by_group, *observed):
+def exchange(cap, spectrum, courant, *observed):
     vmem = pl.BlockSpec(memory_space=pltpu.VMEM)
     lists = -(-cap // LANES)
     return pl.pallas_call(
         functools.partial(exchange_kernel, cap),
         out_shape=(
-            jax.ShapeDtypeStruct((CELLS + 16, LANES), f32),
-            jax.ShapeDtypeStruct((144, LANES), f32),
+            jax.ShapeDtypeStruct((CELLS, LANES), f32),
+            jax.ShapeDtypeStruct((32, LANES), f32),
+            jax.ShapeDtypeStruct((ROWS, COLS), f32),
             jax.ShapeDtypeStruct((4 * cap, LANES), f32),
-            jax.ShapeDtypeStruct((GROUPS, ROWS, LANES), f32),
-            jax.ShapeDtypeStruct((GROUPS, ROWS, LANES), f32),
-            jax.ShapeDtypeStruct((4, GROUPS, GROUP), i32),
+            jax.ShapeDtypeStruct((GROUPS, GROUP), i32),
+            jax.ShapeDtypeStruct((2 * GROUPS, GROUP), f32),
         ),
-        in_specs=[pl.BlockSpec(memory_space=pl.ANY)] * 8,
+        in_specs=[pl.BlockSpec(memory_space=pl.ANY)] * 7,
         out_specs=(vmem,) * 6,
         scratch_shapes=[
+            pltpu.VMEM((CELLS + 16, LANES), f32),
+            pltpu.VMEM((112, LANES), f32),
+            pltpu.VMEM((GROUPS, ROWS, LANES), f32),
+            pltpu.VMEM((GROUPS, ROWS, LANES), f32),
+            pltpu.VMEM((3, GROUPS, GROUP), i32),
+            pltpu.SMEM((3, GROUPS, GROUP), i32),
             pltpu.SMEM((2 * GROUPS, GROUP), f32),
             pltpu.VMEM((2, SPEC), f32),
-            pltpu.VMEM((2 * GROUPS, GROUP), f32),
             pltpu.VMEM((1, 256), i32),
             pltpu.VMEM((1, 256), i32),
             pltpu.VMEM((1, 256), f32),
@@ -643,99 +720,44 @@
             vmem_limit_bytes=30 * 2**20,
         ),
         name=f"exchange_{cap}",
-    )(spectrum, courant, by_group, *observed)
+    )(spectrum, courant, *observed)
 
 
 def update_kernel(
-    by_group,
-    cells,
-    tables,
-    rows,
-    cols_west,
-    cols_east,
-    plan,
-    out,
-    increment,
-    steps,
-    sem,
+    partial, rim_tables, increments, rows, places, speeds, out, increment, place, speed, sems
 ):
     step = pl.program_id(0)
 
     @pl.when(step == 0)
     def _():
-        copy = pltpu.make_async_copy(plan, steps, sem)
-        copy.start()
-        increment[:, 0:LANES] = tables[112:120, :]
-        increment[:, LANES:COLS] = tables[120:128, :]
-        copy.wait()
-
-    lane = lax.broadcasted_iota(i32, (ROWS, LANES), 1)
-    sub = lax.broadcasted_iota(i32, (ROWS, LANES), 0)
-    plain = tables[0:8, :], tables[8:16, :]
-
-    def eight(ref, first):
-        return ref[pl.ds(pl.multiple_of(first, 8), 8), :]
-
-    def some(part, carry):
-        for u in range(MEMBERS):
-            one(part * MEMBERS + u)
-        return carry
-
-    def one(u):
-        at = 8 + (step * GROUP + u) * 16
-        cell = eight(cells, at), eight(cells, at + 8)
-        speed = jnp.full((ROWS, LANES), by_group[step, u])
-        back = speed < 0.0
-        flow = [
-            cell[half]
-            * jnp.where(
-                back,
-                tables[32 + 8 * half : 40 + 8 * half, :],
-                tables[16 + 8 * half : 24 + 8 * half, :],
-            )
-            for half in range(2)
+        copies = [
+            pltpu.make_async_copy(places, place, sems.at[0]),
+            pltpu.make_async_copy(speeds, speed, sems.at[1]),
         ]
-        shift = steps[0, step, u]
-        moved = pltpu.roll(flow[0], shift, 1), pltpu.roll(flow[1], shift, 1)
-        rim = pltpu.roll(jnp.where(back, rims[1], rims[0]), steps[1, step, u], 1)
-        at_edge = lane == jnp.where(back, LANES - 1, 0)
-        came = (
-            jnp.where(at_edge, jnp.where(back, moved[1], rim), moved[0]),
-            jnp.where(at_edge, jnp.where(back, rim, moved[0]), moved[1]),
-        )
-        speed = jnp.abs(speed)
-
-        slow = jnp.full((ROWS, LANES), by_group[GROUPS + step, u])
+        for copy in copies:
+            copy.start()
+        increment[...] = increments[...]
+        for copy in copies:
+            copy.wait()
+
+    for u in range(GROUP):
+        at = (step * GROUP + u) * 16
+        slow = jnp.full((ROWS, LANES), speed[GROUPS + step, u])
         down = slow < 0.0
-        at_row = sub == jnp.where(down, ROWS - 1, 0)
         slow = jnp.abs(slow)
-        near = steps[2, step, u]
-        place = steps[3, step, u]
+        line = place[step, u]
         for half in range(2):
-            beyond = jnp.where(
-                at_row,
-                jnp.broadcast_to(rows[pl.ds(place + half, 1), :], (ROWS, LANES)),
-                cells[pl.ds(near + 8 * half, 8), :],
-            )
             first = 8 * half
             way = jnp.where(
-                down, tables[64 + first : 72 + first, :], tables[48 + first : 56 + first, :]
+                down, rim_tables[16 + first : 24 + first, :], rim_tables[first : first + 8, :]
             )
-            way_in = jnp.where(
-                down, tables[96 + first : 104 + first, :], tables[80 + first : 88 + first, :]
+            row = jnp.broadcast_to(rows[pl.ds(line + half, 1), :], (ROWS, LANES))
+            out[u * 16 + first : u * 16 + first + 8, :] = (
+                partial[pl.ds(pl.multiple_of(at + first, 8), 8), :] + slow * (row * way)
             )
-            gone = cell[half] * way - beyond * way_in
-            out[pl.ds(pl.multiple_of(u * 16 + first, 8), 8), :] = (
-                cell[half] * plain[half]
-                - speed * (flow[half] - came[half])
-                - slow * gone
-            )
-
-    rims = cols_west[step] * tables[128:136, :], cols_east[step] * tables[136:144, :]
-    lax.fori_loop(0, GROUP // MEMBERS, some, 0)
-
-
-def update(cap, by_group, cells, tables, rows, cols_west, cols_east, plan):
+
+
+def update(cap, *sent):
     vmem = pl.BlockSpec(memory_space=pltpu.VMEM)
     return pl.pallas_call(
         update_kernel,
@@ -744,20 +766,21 @@
             jax.ShapeDtypeStruct((CELLS, LANES), f32),
             jax.ShapeDtypeStruct((ROWS, COLS), f32),
         ),
-        in_specs=[pl.BlockSpec(memory_space=pltpu.SMEM)] + [vmem] * 6,
+        in_specs=[vmem] * 6,
         out_specs=(
             pl.BlockSpec((GROUP * 16, LANES), lambda i: (i, 0)),
             pl.BlockSpec((ROWS, COLS), lambda i: (0, 0)),
         ),
         scratch_shapes=[
-            pltpu.SMEM((4, GROUPS, GROUP), i32),
-            pltpu.SemaphoreType.DMA,
+            pltpu.SMEM((GROUPS, GROUP), i32),
+            pltpu.SMEM((2 * GROUPS, GROUP), f32),
+            pltpu.SemaphoreType.DMA((2,)),
         ],
         compiler_params=pltpu.CompilerParams(
             dimension_semantics=("arbitrary",), vmem_limit_bytes=24 * 2**20
         ),
         name=f"update_{cap}",
-    )(by_group, cells, tables, rows, cols_west, cols_east, plan)
+    )(*sent)
 
 
 def body(spectrum, sea_mask, courant, obs_tile, obs_cell, obs_value, obs_error):
@@ -769,19 +792,14 @@
         obs_error.reshape(1, -1),
         sea_mask,
     )
-    by_group = courant.reshape(2 * GROUPS, GROUP)
     south = jnp.sum((courant[1] < 0.0).astype(i32))
     fits = jnp.maximum(south, SPEC - south) <= CAP_HALF
 
     def run(cap):
-        sent = exchange(
-            cap, halves.reshape(CELLS, LANES), courant, by_group, *observed
-        )
-        return update(cap, by_group, *sent)
-
-    updated, increment = lax.cond(
-        fits, lambda: run(CAP_HALF), lambda: run(CAP_ALL)
-    )
+        sent = exchange(cap, halves.reshape(CELLS, LANES), courant, *observed)
+        return update(cap, *sent)
+
+    updated, increment = lax.cond(fits, lambda: run(CAP_HALF), lambda: run(CAP_ALL))
     updated = updated.reshape(SPEC, 2, ROWS, LANES).transpose(0, 2, 1, 3)
     return updated.reshape(SPEC, ROWS, COLS), increment
 

time: 49.8 us -> 45.3 us (0.910)
  Pallas kernels: 44.8 us -> 41.5 us
  local copies, waits for them, and re-layouts: 0.79 us -> 0 us
    pallas_call x1, Pallas kernels: 14.8 us -> 9.63 us  [update(): pl.pallas_call(update_kernel, grid=(GROUPS,), out_shape=(jax.ShapeDtypeSt...]
    pallas_call x1, Pallas kernels: 29.9 us -> 31.8 us  [exchange(): pl.pallas_call(functools.partial(exchange_kernel, cap), out_shape=(jax.Sh...]
    reshape x1 -> x0, local copies, waits for them, and re-layouts: 0.79 us -> none  [body(): by_group = courant.reshape(2 * GROUPS, GROUP)]
where the time goes in v3:
time: 45.3 us; the launch traced here: 44.8 us
  Pallas kernels  41.5 us (92%)
  between operations  1.93 us (4%)
  other arithmetic  1.36 us (3%)
    pallas_call x1, Pallas kernels, exchange(): pl.pallas_call(functools.partial(exchange_kernel, cap), out_shape=(jax.Sh...  31.8 us
    pallas_call x1, Pallas kernels, update(): pl.pallas_call(update_kernel, grid=(GROUPS,), out_shape=(jax.ShapeDtypeSt...  9.63 us
    reduce_sum x1, other arithmetic, body(): south = jnp.sum((courant[1] < 0.0).astype(i32))  1.36 us

profile of v3, /device:TPU:0, one launch (start us, length us, event | category | flops | bytes accessed | tf_op | source)
XLA Modules:
  0.0 44.8 jit_solution(15424926289432818510)
XLA Ops:
  0.6 1.4 %fusion = s32[]{:T(128)} fusion(f32[2,1296]{1,0:T(2,128)} %param.11), kind=kLoop, calls=%fused_computation.1 | loop fusion | flops 3887 | bytes 5188 | tf_op jit(solution)/shard_map/reduce_sum | solution.py:795
  3.3 41.5 %conditional.1 = ((f32[20736,128]{1,0:T(8,128)}, f32[8,256]{1,0:T(8,128)})) conditional(s32[]{:T(128)} %convert_element_type.8, (f32[1296,2,8,128]{3,2,1,0:T(8,128)}, f32[2,1296]{1,0:T(2,128)}, s32[1,256]{1,0:T(1,128)}, s32[1,256]{1,0:T(1,128)}, f32[1,256]{1,0:T(1,128)}, /*index=5*/f32[1,256]{1,0:T(1,128)}, s32[8,256]{1,0:T(8,128)}) %tuple.28, ...), branch_computations={%region_1.0_spmd, %region_2.0_spmd} | conditional | bytes 8 | solution.py:802
  3.3 31.8 %exchange_704.1 = (f32[20736,128]{1,0:T(8,128)S(1)}, f32[32,128]{1,0:T(8,128)S(1)}, f32[8,256]{1,0:T(8,128)S(1)}, f32[2816,128]{1,0:T(8,128)S(1)}, s32[18,72]{1,0:T(8,128)S(1)}, /*index=5*/f32[36,72]{1,0:T(8,128)S(1)}) custom-call(f32[20736,128]{1,0:T(8,128)} %bitcast.17, f32[2,1296]{1,0:T(2,128)} %get-tuple-element.42.courant, ...), custom_call_target="tpu_custom_call" | custom-call | tf_op jit(solution)/shard_map/cond/branch_1_fun/exchange_704/pallas_call | solution.py:670
  35.1 9.6 %update_704.1 = (f32[20736,128]{1,0:T(8,128)}, f32[8,256]{1,0:T(8,128)}) custom-call(f32[20736,128]{1,0:T(8,128)S(1)} %get-tuple-element.48.partial, f32[32,128]{1,0:T(8,128)S(1)} %get-tuple-element.49.rim_tables, f32[8,256]{1,0:T(8,128)S(1)} %get-tuple-element.50.increments, f32[2816,128]{1,0:T(8,128)S(1)} %get-tuple-element.51.rows, ...), custom_call_target="tpu_custom_call" | custom-call | tf_op jit(solution)/shard_map/cond/branch_1_fun/update_704/pallas_call | solution.py:762

commit v4 on v3

--- a/solution.py
+++ b/solution.py
@@ -149,51 +149,8 @@
         device_id_type=LOGICAL,
     )
 
-    for copy in small[0:4]:
-        copy.wait()
-    owner = own_tile[...]
-    owner_lat = lax.shift_right_logical(owner, 5)
-    owner_lon = lax.bitwise_and(owner, 31)
-    tiles = lax.broadcasted_iota(i32, (DEV, 256), 0)
-    hit = jnp.where(tiles == owner, 1.0, 0.0)
-    before = jnp.where(
-        lax.broadcasted_iota(i32, (256, 256), 0)
-        < lax.broadcasted_iota(i32, (256, 256), 1),
-        1.0,
-        0.0,
-    )
-    earlier = lax.dot_general(
-        hit.astype(bf16), before.astype(bf16), NN, preferred_element_type=f32
-    )
-    rank = jnp.sum(hit * earlier, axis=0, keepdims=True).astype(i32)
-    slot = owner_lat * 8 + rank
-    slots = lax.broadcasted_iota(i32, (32, 256), 0)
-    in_slot = slots == slot
-    to_lon = jnp.where(slots == owner_lon, 1.0, 0.0).astype(bf16)
-    zero = jnp.zeros((32, 256), f32)
-    weights = 1.0 / own_error[...]
-    spread = jnp.concatenate(
-        [
-            jnp.where(in_slot, value, zero)
-            for value in (weights * own_value[...], weights, own_cell[...].astype(f32))
-        ]
-        + [zero],
-        axis=0,
-    )
-    packed = jnp.zeros((LON, LANES), f32)
-    for piece in thirds(spread):
-        packed = packed + lax.dot_general(
-            to_lon, piece, NT, preferred_element_type=f32
-        )
-    outbox[...] = packed
-
     for copy in small[4:6]:
         copy.wait()
-    for group in range(GROUPS):
-        for way in range(2):
-            own_groups[way * GROUPS + group : way * GROUPS + group + 1, :] = own_courant[
-                way : way + 1, group * GROUP : (group + 1) * GROUP
-            ]
     number = lax.broadcasted_iota(i32, (16, LANES), 0) * LANES + lax.broadcasted_iota(
         i32, (16, LANES), 1
     )
@@ -258,6 +215,126 @@
     to_scalars = pltpu.make_async_copy(listed, picks, list_sem)
     to_scalars.start()
 
+    def pick_chunk(number):
+        def pick(turn, carry):
+            for u in range(8):
+                at = number * CHUNK + turn * 8 + u
+                line = lax.div(number, 2)
+                spot = lax.rem(number, 2) * CHUNK + turn * 8 + u
+                first = 8 + 16 * picks[0, line, spot]
+                going_north[pl.ds(2 * at, 1), :] = cells[pl.ds(first + 7, 1), :]
+                going_north[pl.ds(2 * at + 1, 1), :] = cells[pl.ds(first + 15, 1), :]
+                first = 8 + 16 * picks[1, line, spot]
+                going_south[pl.ds(2 * at, 1), :] = cells[pl.ds(first, 1), :]
+                going_south[pl.ds(2 * at + 1, 1), :] = cells[pl.ds(first + 8, 1), :]
+            return carry
+
+        lax.fori_loop(0, CHUNK // 8, pick, 0)
+
+    def north_copy(first, count):
+        return pltpu.make_async_remote_copy(
+            src_ref=going_north.at[pl.ds(first, count)],
+            dst_ref=rows.at[pl.ds(first, count)],
+            send_sem=row_sems.at[0],
+            recv_sem=row_sems.at[1],
+            device_id=(lat + 1, lon),
+            device_id_type=MESH,
+        )
+
+    def south_copy(first, count):
+        return pltpu.make_async_remote_copy(
+            src_ref=going_south.at[pl.ds(first, count)],
+            dst_ref=rows.at[pl.ds(2 * cap + first, count)],
+            send_sem=row_sems.at[2],
+            recv_sem=row_sems.at[3],
+            device_id=(lat - 1, lon),
+            device_id_type=MESH,
+        )
+
+    def send_chunk(number):
+        first = pl.multiple_of(number * (2 * CHUNK), 2 * CHUNK)
+
+        @pl.when(lat < LAT - 1)
+        def _():
+            north_copy(first, 2 * CHUNK).start()
+
+        @pl.when(lat > 0)
+        def _():
+            south_copy(first, 2 * CHUNK).start()
+
+    for copy in loads:
+        copy.wait()
+    to_scalars.wait()
+    pick_chunk(0)
+    pick_chunk(1)
+    pick_chunk(2)
+    pl.semaphore_wait(barrier, DEV - 1)
+    for number in range(3):
+        send_chunk(number)
+
+    for copy in small[0:4]:
+        copy.wait()
+    owner = own_tile[...]
+    owner_lat = lax.shift_right_logical(owner, 5)
+    owner_lon = lax.bitwise_and(owner, 31)
+    tiles = lax.broadcasted_iota(i32, (DEV, 256), 0)
+    hit = jnp.where(tiles == owner, 1.0, 0.0)
+    before = jnp.where(
+        lax.broadcasted_iota(i32, (256, 256), 0)
+        < lax.broadcasted_iota(i32, (256, 256), 1),
+        1.0,
+        0.0,
+    )
+    earlier = lax.dot_general(
+        hit.astype(bf16), before.astype(bf16), NN, preferred_element_type=f32
+    )
+    rank = jnp.sum(hit * earlier, axis=0, keepdims=True).astype(i32)
+    slot = owner_lat * 8 + rank
+    slots = lax.broadcasted_iota(i32, (32, 256), 0)
+    in_slot = slots == slot
+    to_lon = jnp.where(slots == owner_lon, 1.0, 0.0).astype(bf16)
+    zero = jnp.zeros((32, 256), f32)
+    weights = 1.0 / own_error[...]
+    spread = jnp.concatenate(
+        [
+            jnp.where(in_slot, value, zero)
+            for value in (weights * own_value[...], weights, own_cell[...].astype(f32))
+        ]
+        + [zero],
+        axis=0,
+    )
+    packed = jnp.zeros((LON, LANES), f32)
+    for piece in thirds(spread):
+        packed = packed + lax.dot_general(
+            to_lon, piece, NT, preferred_element_type=f32
+        )
+    outbox[...] = packed
+
+    def post(turn, carry):
+        for u in range(7):
+            peer = lax.rem(me + (turn * 7 + u + 1), DEV)
+            post_to(peer)
+        return carry
+
+    def post_to(peer):
+        pltpu.make_async_remote_copy(
+            src_ref=outbox.at[pl.ds(lax.rem(peer, LON), 1)],
+            dst_ref=inbox.at[pl.ds(me, 1)],
+            send_sem=box_sems.at[0],
+            recv_sem=box_sems.at[1],
+            device_id=peer,
+            device_id_type=LOGICAL,
+        ).start()
+
+    lax.fori_loop(0, 18, post, 0)
+    post_to(lax.rem(me + DEV - 1, DEV))
+    inbox[pl.ds(me, 1), :] = outbox[pl.ds(lon, 1), :]
+
+    for group in range(GROUPS):
+        for way in range(2):
+            own_groups[way * GROUPS + group : way * GROUPS + group + 1, :] = own_courant[
+                way : way + 1, group * GROUP : (group + 1) * GROUP
+            ]
     to_east = own_groups[0:GROUPS, :] < 0.0
     to_north = own_groups[GROUPS : 2 * GROUPS, :] < 0.0
     shape = (GROUPS, GROUP)
@@ -299,83 +376,8 @@
     cells[0:8, :] = jnp.zeros((8, LANES), f32)
     cells[8 + CELLS : 16 + CELLS, :] = jnp.zeros((8, LANES), f32)
 
-    def pick_chunk(number):
-        def pick(turn, carry):
-            for u in range(8):
-                at = number * CHUNK + turn * 8 + u
-                line = lax.div(number, 2)
-                spot = lax.rem(number, 2) * CHUNK + turn * 8 + u
-                first = 8 + 16 * picks[0, line, spot]
-                going_north[pl.ds(2 * at, 1), :] = cells[pl.ds(first + 7, 1), :]
-                going_north[pl.ds(2 * at + 1, 1), :] = cells[pl.ds(first + 15, 1), :]
-                first = 8 + 16 * picks[1, line, spot]
-                going_south[pl.ds(2 * at, 1), :] = cells[pl.ds(first, 1), :]
-                going_south[pl.ds(2 * at + 1, 1), :] = cells[pl.ds(first + 8, 1), :]
-            return carry
-
-        lax.fori_loop(0, CHUNK // 8, pick, 0)
-
-    def north_copy(first, count):
-        return pltpu.make_async_remote_copy(
-            src_ref=going_north.at[pl.ds(first, count)],
-            dst_ref=rows.at[pl.ds(first, count)],
-            send_sem=row_sems.at[0],
-            recv_sem=row_sems.at[1],
-            device_id=(lat + 1, lon),
-            device_id_type=MESH,
-        )
-
-    def south_copy(first, count):
-        return pltpu.make_async_remote_copy(
-            src_ref=going_south.at[pl.ds(first, count)],
-            dst_ref=rows.at[pl.ds(2 * cap + first, count)],
-            send_sem=row_sems.at[2],
-            recv_sem=row_sems.at[3],
-            device_id=(lat - 1, lon),
-            device_id_type=MESH,
-        )
-
-    def send_chunk(number):
-        first = pl.multiple_of(number * (2 * CHUNK), 2 * CHUNK)
-
-        @pl.when(lat < LAT - 1)
-        def _():
-            north_copy(first, 2 * CHUNK).start()
-
-        @pl.when(lat > 0)
-        def _():
-            south_copy(first, 2 * CHUNK).start()
-
-    pl.semaphore_wait(barrier, DEV - 1)
-    def post(turn, carry):
-        for u in range(7):
-            peer = lax.rem(me + (turn * 7 + u + 1), DEV)
-            post_to(peer)
-        return carry
-
-    def post_to(peer):
-        pltpu.make_async_remote_copy(
-            src_ref=outbox.at[pl.ds(lax.rem(peer, LON), 1)],
-            dst_ref=inbox.at[pl.ds(me, 1)],
-            send_sem=box_sems.at[0],
-            recv_sem=box_sems.at[1],
-            device_id=peer,
-            device_id_type=LOGICAL,
-        ).start()
-
-    lax.fori_loop(0, 18, post, 0)
-    post_to(lax.rem(me + DEV - 1, DEV))
-    inbox[pl.ds(me, 1), :] = outbox[pl.ds(lon, 1), :]
-
-    for copy in loads:
-        copy.wait()
-    to_scalars.wait()
     for copy in scalars:
         copy.wait()
-    pick_chunk(0)
-    pick_chunk(1)
-    send_chunk(0)
-    send_chunk(1)
 
     lane = lax.broadcasted_iota(i32, (ROWS, LANES), 1)
     blank = jnp.zeros((ROWS, LANES), f32)
@@ -438,14 +440,15 @@
     send_west.start()
     send_east.start()
 
-    pick_chunk(2)
+    pick_chunk(3)
 
     def forward(number, carry):
         pick_chunk(number)
         send_chunk(number - 1)
         return carry
 
-    lax.fori_loop(3, chunks, forward, 0)
+    early = chunks * 7 // 11
+    lax.fori_loop(4, early, forward, 0)
 
     @pl.when(lat == 0)
     def _():
@@ -455,7 +458,26 @@
     def _():
         rows[2 * cap : 4 * cap, :] = jnp.zeros((2 * cap, LANES), f32)
 
-    send_chunk(chunks - 1)
+    def rim_copies(first, sems):
+        part = pl.ds(first, 2)
+        return (
+            pltpu.make_async_remote_copy(
+                src_ref=fields.at[part, pl.ds(0, NROW), pl.ds(0, LANES)],
+                dst_ref=near_east.at[part],
+                send_sem=rim_sems.at[sems],
+                recv_sem=rim_sems.at[sems + 1],
+                device_id=(lat, west),
+                device_id_type=MESH,
+            ),
+            pltpu.make_async_remote_copy(
+                src_ref=fields.at[part, pl.ds(0, NROW), pl.ds(LANES, LANES)],
+                dst_ref=near_west.at[part],
+                send_sem=rim_sems.at[sems + 2],
+                recv_sem=rim_sems.at[sems + 3],
+                device_id=(lat, east),
+                device_id_type=MESH,
+            ),
+        )
 
     got = pl.ds(0, DEV - 1)
     pltpu.make_async_copy(inbox.at[got], inbox.at[got], box_sems.at[1]).wait()
@@ -498,32 +520,21 @@
     three = fields.at[pl.ds(2, 2), pl.ds(0, NROW - ROWS), pl.ds(0, COLS)]
     pltpu.make_async_copy(three, three, lat_sems.at[1]).wait()
     pltpu.make_async_copy(three, three, lat_sems.at[0]).wait()
+    coast_rims = rim_copies(2, 0)
+    for copy in coast_rims:
+        copy.start()
     height = fields[2, :, 0:COLS]
     ocean = fields[3, :, 0:COLS]
     weight = fields[1, :, 0:COLS] * ocean
     fields[0, :, 0:COLS] = (fields[0, :, 0:COLS] - height * fields[1, :, 0:COLS]) * ocean
     fields[1, :, 0:COLS] = weight
-
-    rim_west = pltpu.make_async_remote_copy(
-        src_ref=fields.at[pl.ds(0, 4), pl.ds(0, NROW), pl.ds(0, LANES)],
-        dst_ref=near_east,
-        send_sem=rim_sems.at[0],
-        recv_sem=rim_sems.at[1],
-        device_id=(lat, west),
-        device_id_type=MESH,
-    )
-    rim_east = pltpu.make_async_remote_copy(
-        src_ref=fields.at[pl.ds(0, 4), pl.ds(0, NROW), pl.ds(LANES, LANES)],
-        dst_ref=near_west,
-        send_sem=rim_sems.at[2],
-        recv_sem=rim_sems.at[3],
-        device_id=(lat, east),
-        device_id_type=MESH,
-    )
-    rim_west.start()
-    rim_east.start()
-    rim_west.wait()
-    rim_east.wait()
+    field_rims = rim_copies(0, 4)
+    for copy in field_rims:
+        copy.start()
+    lax.fori_loop(early, chunks, forward, 0)
+    send_chunk(chunks - 1)
+    for copy in coast_rims + field_rims:
+        copy.wait()
     lane = lax.broadcasted_iota(i32, (NROW, LANES), 1)
     for number, filler in enumerate((0.0, 0.0, 1.0, 0.0)):
         fields[number, :, COLS:EXT] = jnp.where(
@@ -677,7 +688,7 @@
             jax.ShapeDtypeStruct((GROUPS, GROUP), i32),
             jax.ShapeDtypeStruct((2 * GROUPS, GROUP), f32),
         ),
-        in_specs=[pl.BlockSpec(memory_space=pl.ANY)] * 7,
+        in_specs=[pl.BlockSpec(memory_space=pltpu.HBM)] * 7,
         out_specs=(vmem,) * 6,
         scratch_shapes=[
             pltpu.VMEM((CELLS + 16, LANES), f32),
@@ -711,7 +722,7 @@
             pltpu.SemaphoreType.DMA((2,)),
             pltpu.SemaphoreType.DMA((2,)),
             pltpu.SemaphoreType.DMA((4,)),
-            pltpu.SemaphoreType.DMA((4,)),
+            pltpu.SemaphoreType.DMA((8,)),
             pltpu.SemaphoreType.DMA((4,)),
         ],
         compiler_params=pltpu.CompilerParams(
@@ -724,61 +735,83 @@
 
 
 def update_kernel(
-    partial, rim_tables, increments, rows, places, speeds, out, increment, place, speed, sems
+    partial,
+    rim_tables,
+    increments,
+    rows,
+    places,
+    speeds,
+    out,
+    increment,
+    stage,
+    place,
+    speed,
+    sems,
+    out_sems,
 ):
-    step = pl.program_id(0)
-
-    @pl.when(step == 0)
-    def _():
-        copies = [
-            pltpu.make_async_copy(places, place, sems.at[0]),
-            pltpu.make_async_copy(speeds, speed, sems.at[1]),
-        ]
-        for copy in copies:
-            copy.start()
-        increment[...] = increments[...]
-        for copy in copies:
-            copy.wait()
-
-    for u in range(GROUP):
-        at = (step * GROUP + u) * 16
-        slow = jnp.full((ROWS, LANES), speed[GROUPS + step, u])
-        down = slow < 0.0
-        slow = jnp.abs(slow)
-        line = place[step, u]
-        for half in range(2):
-            first = 8 * half
-            way = jnp.where(
-                down, rim_tables[16 + first : 24 + first, :], rim_tables[first : first + 8, :]
-            )
-            row = jnp.broadcast_to(rows[pl.ds(line + half, 1), :], (ROWS, LANES))
-            out[u * 16 + first : u * 16 + first + 8, :] = (
-                partial[pl.ds(pl.multiple_of(at + first, 8), 8), :] + slow * (row * way)
-            )
+    copies = [
+        pltpu.make_async_copy(places, place, sems.at[0]),
+        pltpu.make_async_copy(speeds, speed, sems.at[1]),
+    ]
+    for copy in copies:
+        copy.start()
+    increment[...] = increments[...]
+    for copy in copies:
+        copy.wait()
+    size = GROUP * 16
+
+    def store(group):
+        part = pl.ds(pl.multiple_of(group * size, size), size)
+        return pltpu.make_async_copy(stage.at[part], out.at[part], out_sems.at[group])
+
+    def finish(step):
+        for u in range(GROUP):
+            at = (step * GROUP + u) * 16
+            slow = jnp.full((ROWS, LANES), speed[GROUPS + step, u])
+            down = slow < 0.0
+            slow = jnp.abs(slow)
+            line = place[step, u]
+            for half in range(2):
+                first = 8 * half
+                way = jnp.where(
+                    down,
+                    rim_tables[16 + first : 24 + first, :],
+                    rim_tables[first : first + 8, :],
+                )
+                row = jnp.broadcast_to(rows[pl.ds(line + half, 1), :], (ROWS, LANES))
+                here = pl.ds(pl.multiple_of(at + first, 8), 8)
+                stage[here, :] = partial[here, :] + slow * (row * way)
+
+    finish(0)
+
+    def follow(step, carry):
+        finish(step)
+        store(step - 1).start()
+        return carry
+
+    lax.fori_loop(1, GROUPS, follow, 0)
+    store(GROUPS - 1).start()
+    lax.fori_loop(0, GROUPS, lambda g, carry: (store(g).wait(), carry)[1], 0)
 
 
 def update(cap, *sent):
     vmem = pl.BlockSpec(memory_space=pltpu.VMEM)
     return pl.pallas_call(
         update_kernel,
-        grid=(GROUPS,),
         out_shape=(
             jax.ShapeDtypeStruct((CELLS, LANES), f32),
             jax.ShapeDtypeStruct((ROWS, COLS), f32),
         ),
         in_specs=[vmem] * 6,
-        out_specs=(
-            pl.BlockSpec((GROUP * 16, LANES), lambda i: (i, 0)),
-            pl.BlockSpec((ROWS, COLS), lambda i: (0, 0)),
-        ),
+        out_specs=(pl.BlockSpec(memory_space=pl.ANY), vmem),
         scratch_shapes=[
+            pltpu.VMEM((CELLS, LANES), f32),
             pltpu.SMEM((GROUPS, GROUP), i32),
             pltpu.SMEM((2 * GROUPS, GROUP), f32),
             pltpu.SemaphoreType.DMA((2,)),
+            pltpu.SemaphoreType.DMA((GROUPS,)),
         ],
-        compiler_params=pltpu.CompilerParams(
-            dimension_semantics=("arbitrary",), vmem_limit_bytes=24 * 2**20
-        ),
+        compiler_params=pltpu.CompilerParams(vmem_limit_bytes=20 * 2**20),
         name=f"update_{cap}",
     )(*sent)
 
@@ -792,8 +825,10 @@
         obs_error.reshape(1, -1),
         sea_mask,
     )
-    south = jnp.sum((courant[1] < 0.0).astype(i32))
-    fits = jnp.maximum(south, SPEC - south) <= CAP_HALF
+    over = lax.reduce(
+        (courant[1] < 0.0).astype(i32), jnp.int32(CAP_HALF - SPEC), lax.add, (0,)
+    )
+    fits = over.astype(jnp.uint32) <= 2 * CAP_HALF - SPEC
 
     def run(cap):
         sent = exchange(cap, halves.reshape(CELLS, LANES), courant, *observed)

time: 45.3 us -> 53.3 us (1.18)
  Pallas kernels: 41.5 us -> 49.8 us
  between operations: 1.93 us -> 1.28 us
    pallas_call x1, Pallas kernels: 31.8 us -> 43.8 us  [exchange(): pl.pallas_call(functools.partial(exchange_kernel, cap), out_shape=(jax.Sh...]
    pallas_call x1, Pallas kernels: 9.63 us -> 5.95 us  [update(): pl.pallas_call(update_kernel, out_shape=(jax.ShapeDtypeStruct((CELLS, LAN...]
    another operation x0 -> x1, other arithmetic: none -> 1.36 us  [body(): lax.reduce((courant[1] < 0.0).astype(i32), jnp.int32(CAP_HALF - SPEC), la...]
    reduce_sum x1 -> x0, other arithmetic: 1.36 us -> none  [body(): south = jnp.sum((courant[1] < 0.0).astype(i32))]
where the time goes in v4:
time: 53.3 us; the launch traced here: 52.4 us
  Pallas kernels  49.8 us (93%)
  other arithmetic  1.36 us (3%)
  between operations  1.28 us (2%)
    pallas_call x1, Pallas kernels, exchange(): pl.pallas_call(functools.partial(exchange_kernel, cap), out_shape=(jax.Sh...  43.8 us
    pallas_call x1, Pallas kernels, update(): pl.pallas_call(update_kernel, out_shape=(jax.ShapeDtypeStruct((CELLS, LAN...  5.95 us
    another operation x1, other arithmetic, body(): lax.reduce((courant[1] < 0.0).astype(i32), jnp.int32(CAP_HALF - SPEC), la...  1.36 us

profile of v4, /device:TPU:0, one launch (start us, length us, event | category | flops | bytes accessed | tf_op | source)
XLA Modules:
  0.0 52.4 jit_solution(9467516796395825122)
XLA Ops:
  0.6 1.4 %fusion = s32[]{:T(128)} fusion(f32[2,1296]{1,0:T(2,128)} %param.11), kind=kLoop, calls=%fused_computation.1 | loop fusion | flops 3887 | bytes 5188 | tf_op jit(solution)/shard_map/reduce | solution.py:828
  2.6 49.8 %conditional.1 = ((f32[20736,128]{1,0:T(8,128)}, f32[8,256]{1,0:T(8,128)})) conditional(s32[]{:T(128)} %convert_element_type.12, (f32[1296,2,8,128]{3,2,1,0:T(8,128)}, f32[2,1296]{1,0:T(2,128)}, s32[1,256]{1,0:T(1,128)}, s32[1,256]{1,0:T(1,128)}, f32[1,256]{1,0:T(1,128)}, /*index=5*/f32[1,256]{1,0:T(1,128)}, s32[8,256]{1,0:T(8,128)}) %tuple.28, ...), branch_computations={%region_1.0_spmd, %region_2.0_spmd} | conditional | bytes 8 | solution.py:837
  2.6 43.8 %exchange_1344.1 = (f32[20736,128]{1,0:T(8,128)S(1)}, f32[32,128]{1,0:T(8,128)S(1)}, f32[8,256]{1,0:T(8,128)S(1)}, f32[5376,128]{1,0:T(8,128)S(1)}, s32[18,72]{1,0:T(8,128)S(1)}, /*index=5*/f32[36,72]{1,0:T(8,128)S(1)}) custom-call(f32[20736,128]{1,0:T(8,128)} %bitcast.16, f32[2,1296]{1,0:T(2,128)} %get-tuple-element.29.courant, ...), custom_call_target="tpu_custom_call" | custom-call | tf_op jit(solution)/shard_map/cond/branch_0_fun/exchange_1344/pallas_call | solution.py:681
  46.5 6.0 %update_1344.1 = (f32[20736,128]{1,0:T(8,128)}, f32[8,256]{1,0:T(8,128)}) custom-call(f32[20736,128]{1,0:T(8,128)S(1)} %get-tuple-element.35.partial, f32[32,128]{1,0:T(8,128)S(1)} %get-tuple-element.36.rim_tables, f32[8,256]{1,0:T(8,128)S(1)} %get-tuple-element.37.increments, f32[5376,128]{1,0:T(8,128)S(1)} %get-tuple-element.38.rows, ...), custom_call_target="tpu_custom_call" | custom-call | tf_op jit(solution)/shard_map/cond/branch_0_fun/update_1344/pallas_call | solution.py:799

commit v5 on v4

--- a/solution.py
+++ b/solution.py
@@ -825,9 +825,7 @@
         obs_error.reshape(1, -1),
         sea_mask,
     )
-    over = lax.reduce(
-        (courant[1] < 0.0).astype(i32), jnp.int32(CAP_HALF - SPEC), lax.add, (0,)
-    )
+    over = jnp.sum((courant[1] < 0.0).astype(i32)) - (SPEC - CAP_HALF)
     fits = over.astype(jnp.uint32) <= 2 * CAP_HALF - SPEC
 
     def run(cap):

time: 53.3 us -> 42.9 us (0.80); the launches traced: 52.4 us -> 42.8 us
  Pallas kernels: 49.8 us -> 40.1 us
    pallas_call x1, Pallas kernels: 43.8 us -> 34.2 us  [exchange(): pl.pallas_call(functools.partial(exchange_kernel, cap), out_shape=(jax.Sh...]
    reduce_sum x0 -> x1, other arithmetic: none -> 1.36 us  [body(): over = jnp.sum((courant[1] < 0.0).astype(i32)) - (SPEC - CAP_HALF)]
    another operation x1 -> x0, other arithmetic: 1.36 us -> none  [body(): lax.reduce((courant[1] < 0.0).astype(i32), jnp.int32(CAP_HALF - SPEC), la...]
where the time goes in v5:
time: 42.9 us; the launch traced here: 42.8 us
  Pallas kernels  40.1 us (93%)
  other arithmetic  1.36 us (3%)
  between operations  1.28 us (3%)
    pallas_call x1, Pallas kernels, exchange(): pl.pallas_call(functools.partial(exchange_kernel, cap), out_shape=(jax.Sh...  34.2 us
    pallas_call x1, Pallas kernels, update(): pl.pallas_call(update_kernel, out_shape=(jax.ShapeDtypeStruct((CELLS, LAN...  5.95 us
    reduce_sum x1, other arithmetic, body(): over = jnp.sum((courant[1] < 0.0).astype(i32)) - (SPEC - CAP_HALF)  1.36 us

profile of v5, /device:TPU:0, one launch (start us, length us, event | category | flops | bytes accessed | tf_op | source)
XLA Modules:
  0.0 42.8 jit_solution(11275921563211313510)
XLA Ops:
  0.6 1.4 %fusion = s32[]{:T(128)} fusion(f32[2,1296]{1,0:T(2,128)} %param.11), kind=kLoop, calls=%fused_computation.1 | loop fusion | flops 3887 | bytes 5188 | tf_op jit(solution)/shard_map/reduce_sum | solution.py:828
  2.6 40.1 %conditional.1 = ((f32[20736,128]{1,0:T(8,128)}, f32[8,256]{1,0:T(8,128)})) conditional(s32[]{:T(128)} %convert_element_type.12, (f32[1296,2,8,128]{3,2,1,0:T(8,128)}, f32[2,1296]{1,0:T(2,128)}, s32[1,256]{1,0:T(1,128)}, s32[1,256]{1,0:T(1,128)}, f32[1,256]{1,0:T(1,128)}, /*index=5*/f32[1,256]{1,0:T(1,128)}, s32[8,256]{1,0:T(8,128)}) %tuple.28, ...), branch_computations={%region_1.0_spmd, %region_2.0_spmd} | conditional | bytes 8 | solution.py:835
  2.7 34.2 %exchange_704.1 = (f32[20736,128]{1,0:T(8,128)S(1)}, f32[32,128]{1,0:T(8,128)S(1)}, f32[8,256]{1,0:T(8,128)S(1)}, f32[2816,128]{1,0:T(8,128)S(1)}, s32[18,72]{1,0:T(8,128)S(1)}, /*index=5*/f32[36,72]{1,0:T(8,128)S(1)}) custom-call(f32[20736,128]{1,0:T(8,128)} %bitcast.17, f32[2,1296]{1,0:T(2,128)} %get-tuple-element.42.courant, ...), custom_call_target="tpu_custom_call" | custom-call | tf_op jit(solution)/shard_map/cond/branch_1_fun/exchange_704/pallas_call | solution.py:681
  36.8 6.0 %update_704.1 = (f32[20736,128]{1,0:T(8,128)}, f32[8,256]{1,0:T(8,128)}) custom-call(f32[20736,128]{1,0:T(8,128)S(1)} %get-tuple-element.48.partial, f32[32,128]{1,0:T(8,128)S(1)} %get-tuple-element.49.rim_tables, f32[8,256]{1,0:T(8,128)S(1)} %get-tuple-element.50.increments, f32[2816,128]{1,0:T(8,128)S(1)} %get-tuple-element.51.rows, ...), custom_call_target="tpu_custom_call" | custom-call | tf_op jit(solution)/shard_map/cond/branch_1_fun/update_704/pallas_call | solution.py:799

commit v6 on v3

--- a/solution.py
+++ b/solution.py
@@ -445,7 +445,8 @@
         send_chunk(number - 1)
         return carry
 
-    lax.fori_loop(3, chunks, forward, 0)
+    early = chunks * 5 // 11
+    lax.fori_loop(3, early, forward, 0)
 
     @pl.when(lat == 0)
     def _():
@@ -454,8 +455,6 @@
     @pl.when(lat == LAT - 1)
     def _():
         rows[2 * cap : 4 * cap, :] = jnp.zeros((2 * cap, LANES), f32)
-
-    send_chunk(chunks - 1)
 
     got = pl.ds(0, DEV - 1)
     pltpu.make_async_copy(inbox.at[got], inbox.at[got], box_sems.at[1]).wait()
@@ -522,6 +521,8 @@
     )
     rim_west.start()
     rim_east.start()
+    lax.fori_loop(early, chunks, forward, 0)
+    send_chunk(chunks - 1)
     rim_west.wait()
     rim_east.wait()
     lane = lax.broadcasted_iota(i32, (NROW, LANES), 1)
@@ -724,61 +725,83 @@
 
 
 def update_kernel(
-    partial, rim_tables, increments, rows, places, speeds, out, increment, place, speed, sems
+    partial,
+    rim_tables,
+    increments,
+    rows,
+    places,
+    speeds,
+    out,
+    increment,
+    stage,
+    place,
+    speed,
+    sems,
+    out_sems,
 ):
-    step = pl.program_id(0)
-
-    @pl.when(step == 0)
-    def _():
-        copies = [
-            pltpu.make_async_copy(places, place, sems.at[0]),
-            pltpu.make_async_copy(speeds, speed, sems.at[1]),
-        ]
-        for copy in copies:
-            copy.start()
-        increment[...] = increments[...]
-        for copy in copies:
-            copy.wait()
-
-    for u in range(GROUP):
-        at = (step * GROUP + u) * 16
-        slow = jnp.full((ROWS, LANES), speed[GROUPS + step, u])
-        down = slow < 0.0
-        slow = jnp.abs(slow)
-        line = place[step, u]
-        for half in range(2):
-            first = 8 * half
-            way = jnp.where(
-                down, rim_tables[16 + first : 24 + first, :], rim_tables[first : first + 8, :]
-            )
-            row = jnp.broadcast_to(rows[pl.ds(line + half, 1), :], (ROWS, LANES))
-            out[u * 16 + first : u * 16 + first + 8, :] = (
-                partial[pl.ds(pl.multiple_of(at + first, 8), 8), :] + slow * (row * way)
-            )
+    copies = [
+        pltpu.make_async_copy(places, place, sems.at[0]),
+        pltpu.make_async_copy(speeds, speed, sems.at[1]),
+    ]
+    for copy in copies:
+        copy.start()
+    increment[...] = increments[...]
+    for copy in copies:
+        copy.wait()
+    size = GROUP * 16
+
+    def store(group):
+        part = pl.ds(pl.multiple_of(group * size, size), size)
+        return pltpu.make_async_copy(stage.at[part], out.at[part], out_sems.at[group])
+
+    def finish(step):
+        for u in range(GROUP):
+            at = (step * GROUP + u) * 16
+            slow = jnp.full((ROWS, LANES), speed[GROUPS + step, u])
+            down = slow < 0.0
+            slow = jnp.abs(slow)
+            line = place[step, u]
+            for half in range(2):
+                first = 8 * half
+                way = jnp.where(
+                    down,
+                    rim_tables[16 + first : 24 + first, :],
+                    rim_tables[first : first + 8, :],
+                )
+                row = jnp.broadcast_to(rows[pl.ds(line + half, 1), :], (ROWS, LANES))
+                here = pl.ds(pl.multiple_of(at + first, 8), 8)
+                stage[here, :] = partial[here, :] + slow * (row * way)
+
+    finish(0)
+
+    def follow(step, carry):
+        finish(step)
+        store(step - 1).start()
+        return carry
+
+    lax.fori_loop(1, GROUPS, follow, 0)
+    store(GROUPS - 1).start()
+    lax.fori_loop(0, GROUPS, lambda g, carry: (store(g).wait(), carry)[1], 0)
 
 
 def update(cap, *sent):
     vmem = pl.BlockSpec(memory_space=pltpu.VMEM)
     return pl.pallas_call(
         update_kernel,
-        grid=(GROUPS,),
         out_shape=(
             jax.ShapeDtypeStruct((CELLS, LANES), f32),
             jax.ShapeDtypeStruct((ROWS, COLS), f32),
         ),
         in_specs=[vmem] * 6,
-        out_specs=(
-            pl.BlockSpec((GROUP * 16, LANES), lambda i: (i, 0)),
-            pl.BlockSpec((ROWS, COLS), lambda i: (0, 0)),
-        ),
+        out_specs=(pl.BlockSpec(memory_space=pl.ANY), vmem),
         scratch_shapes=[
+            pltpu.VMEM((CELLS, LANES), f32),
             pltpu.SMEM((GROUPS, GROUP), i32),
             pltpu.SMEM((2 * GROUPS, GROUP), f32),
             pltpu.SemaphoreType.DMA((2,)),
+            pltpu.SemaphoreType.DMA((GROUPS,)),
         ],
-        compiler_params=pltpu.CompilerParams(
-            dimension_semantics=("arbitrary",), vmem_limit_bytes=24 * 2**20
-        ),
+        compiler_params=pltpu.CompilerParams(vmem_limit_bytes=20 * 2**20),
         name=f"update_{cap}",
     )(*sent)
 
@@ -792,8 +815,8 @@
         obs_error.reshape(1, -1),
         sea_mask,
     )
-    south = jnp.sum((courant[1] < 0.0).astype(i32))
-    fits = jnp.maximum(south, SPEC - south) <= CAP_HALF
+    over = jnp.sum((courant[1] < 0.0).astype(i32)) - (SPEC - CAP_HALF)
+    fits = over.astype(jnp.uint32) <= 2 * CAP_HALF - SPEC
 
     def run(cap):
         sent = exchange(cap, halves.reshape(CELLS, LANES), courant, *observed)

time: 45.3 us -> 41 us (0.905)
  Pallas kernels: 41.5 us -> 37.8 us
  between operations: 1.93 us -> 1.28 us
    pallas_call x1, Pallas kernels: 9.63 us -> 5.95 us  [update(): pl.pallas_call(update_kernel, out_shape=(jax.ShapeDtypeStruct((CELLS, LAN...]
where the time goes in v6:
time: 41 us; the launch traced here: 40.5 us
  Pallas kernels  37.8 us (92%)
  other arithmetic  1.36 us (3%)
  between operations  1.28 us (3%)
    pallas_call x1, Pallas kernels, exchange(): pl.pallas_call(functools.partial(exchange_kernel, cap), out_shape=(jax.Sh...  31.8 us
    pallas_call x1, Pallas kernels, update(): pl.pallas_call(update_kernel, out_shape=(jax.ShapeDtypeStruct((CELLS, LAN...  5.95 us
    reduce_sum x1, other arithmetic, body(): over = jnp.sum((courant[1] < 0.0).astype(i32)) - (SPEC - CAP_HALF)  1.36 us

profile of v6, /device:TPU:0, one launch (start us, length us, event | category | flops | bytes accessed | tf_op | source)
XLA Modules:
  0.0 40.5 jit_solution(17636565034984305274)
XLA Ops:
  0.6 1.4 %fusion = s32[]{:T(128)} fusion(f32[2,1296]{1,0:T(2,128)} %param.11), kind=kLoop, calls=%fused_computation.1 | loop fusion | flops 3887 | bytes 5188 | tf_op jit(solution)/shard_map/reduce_sum | solution.py:818
  2.6 37.8 %conditional.1 = ((f32[20736,128]{1,0:T(8,128)}, f32[8,256]{1,0:T(8,128)})) conditional(s32[]{:T(128)} %convert_element_type.12, (f32[1296,2,8,128]{3,2,1,0:T(8,128)}, f32[2,1296]{1,0:T(2,128)}, s32[1,256]{1,0:T(1,128)}, s32[1,256]{1,0:T(1,128)}, f32[1,256]{1,0:T(1,128)}, /*index=5*/f32[1,256]{1,0:T(1,128)}, s32[8,256]{1,0:T(8,128)}) %tuple.28, ...), branch_computations={%region_1.0_spmd, %region_2.0_spmd} | conditional | bytes 8 | solution.py:825
  2.7 31.8 %exchange_704.1 = (f32[20736,128]{1,0:T(8,128)S(1)}, f32[32,128]{1,0:T(8,128)S(1)}, f32[8,256]{1,0:T(8,128)S(1)}, f32[2816,128]{1,0:T(8,128)S(1)}, s32[18,72]{1,0:T(8,128)S(1)}, /*index=5*/f32[36,72]{1,0:T(8,128)S(1)}) custom-call(f32[20736,128]{1,0:T(8,128)} %bitcast.17, f32[2,1296]{1,0:T(2,128)} %get-tuple-element.42.courant, ...), custom_call_target="tpu_custom_call" | custom-call | tf_op jit(solution)/shard_map/cond/branch_1_fun/exchange_704/pallas_call | solution.py:671
  34.5 6.0 %update_704.1 = (f32[20736,128]{1,0:T(8,128)}, f32[8,256]{1,0:T(8,128)}) custom-call(f32[20736,128]{1,0:T(8,128)S(1)} %get-tuple-element.48.partial, f32[32,128]{1,0:T(8,128)S(1)} %get-tuple-element.49.rim_tables, f32[8,256]{1,0:T(8,128)S(1)} %get-tuple-element.50.increments, f32[2816,128]{1,0:T(8,128)S(1)} %get-tuple-element.51.rows, ...), custom_call_target="tpu_custom_call" | custom-call | tf_op jit(solution)/shard_map/cond/branch_1_fun/update_704/pallas_call | solution.py:789
